TPU v7x, 1024 devices: a whole 4x8x16 slice. The times are simulated.
1024 devices in a mesh: face: 256 (over y, z, core), sub: 4 (over x).
Axes of the slice: x: 4, y: 8, z: 16, core: 2. Of those that a mesh axis runs over, the one named last changes fastest.
Arguments:
- prognostic: bfloat16 [3, 65536, 16, 128], P(None, ('face', 'sub')), may hold values from -4 to 4
- metric: float32 [4, 65536, 16], P(None, ('face', 'sub')), may hold values from -0.35 to 1.6, as said below
- coriolis: float32 [65536, 16], P(('face', 'sub')), may hold values from -1.5 to 1.5
- node_point: int32 [65536, 16], P(('face', 'sub')), may hold values from 0 to 678, as said below
- send_point: int32 [217088], P(('face', 'sub')), may hold values from 0 to 678, as said below
- recv_point: int32 [217088], P(('face', 'sub')), may hold values from 0 to 678, as said below
Outputs:
- advanced: bfloat16 [3, 65536, 16, 128], P(None, ('face', 'sub'))
Inputs may be any that keep to these rules, and one draw needn't show every extreme that they name: `node_point`: each device's numbers are its 679 local points; element nodes that are the same point of the surface on one device carry the same number. `send_point`: on every device the 212 slots form groups in this order: 7 slots of offset +1, 7 of offset -1, 97 of offset +16, 97 of offset -16, then one slot each of offsets 16 + 1, -16 - 1, 15, 1 - 16. A slot names the sender's point that the device at curve index d + o, taken modulo 1024, shares. Every slot is used. `recv_point`: slot s of device d names the local point that is the same surface point as the sender's slot s, the sender being the device at d minus the slot's group offset modulo 1024. The copies of every shared point are linked between every two devices that hold them. `metric`: entries 0 and 3 lie in [0.6, 1.6], entries 1 and 2 in [-0.35, 0.35].
All inputs are finite; a program needn't handle non-finite values.
Results may differ from a plain program's by a relative error of at most 0.007.
Values sent between devices are 32-bit elements; how exact they have to be, the bound alone decides.
A program may use at most 32 MiB of HBM per device.

v0:
```python
import math

import jax
import jax.numpy as jnp
import numpy as np
from jax import lax
from jax.sharding import PartitionSpec as P

BX = 32
BY = 2
PTS = 679


STEP_SIZE = 0.1


def from_behind(value, axis, steps):
    count = lax.axis_size(axis)
    pairs = [(source, (source + steps) % count) for source in range(count)]
    return lax.ppermute(value, axis, pairs)


def gll_tables():
    abscissa = np.array([-1.0, -math.sqrt(0.2), math.sqrt(0.2), 1.0])
    legendre = 0.5 * (5.0 * abscissa * abscissa * abscissa - 3.0 * abscissa)
    derivative = np.zeros((4, 4))
    for target in range(4):
        for source in range(4):
            if target != source:
                derivative[target, source] = legendre[target] / (
                    legendre[source] * (abscissa[target] - abscissa[source])
                )
    derivative[0, 0] = -3.0
    derivative[3, 3] = 3.0
    weights = np.array([1.0, 5.0, 5.0, 1.0]) / 6.0
    return (derivative, weights)


def along_cols(values, derivative):
    return jnp.einsum("aj,erjl->eral", derivative, values, precision=lax.Precision.HIGHEST)


def along_rows(values, derivative):
    return jnp.einsum("aj,ejcl->eacl", derivative, values, precision=lax.Precision.HIGHEST)


def element_tendency(fields, metric, coriolis):
    elements = fields.shape[1]
    levels = fields.shape[3]
    deriv_table, weight_table = gll_tables()
    derivative = jnp.asarray(deriv_table, dtype=jnp.float32)
    weights = jnp.asarray(weight_table, dtype=jnp.float32)
    shaped = fields.reshape(3, elements, 4, 4, levels)
    veloc_one = shaped[0]
    veloc_two = shaped[1]
    geopot = shaped[2]
    inverse = metric.reshape(4, elements, 4, 4, 1)
    inv_aa = inverse[0]
    inv_ab = inverse[1]
    inv_ba = inverse[2]
    inv_bb = inverse[3]
    jacobian_inv = inv_aa * inv_bb - inv_ab * inv_ba
    energy = 0.5 * (veloc_one * veloc_one + veloc_two * veloc_two) + geopot
    ref_one = along_cols(energy, derivative)
    ref_two = along_rows(energy, derivative)
    grad_one = inv_aa * ref_one + inv_ba * ref_two
    grad_two = inv_ab * ref_one + inv_bb * ref_two
    cov_one = (inv_bb * veloc_one - inv_ba * veloc_two) / jacobian_inv
    cov_two = (inv_aa * veloc_two - inv_ab * veloc_one) / jacobian_inv
    vorticity = jacobian_inv * (along_cols(cov_two, derivative) - along_rows(cov_one, derivative))
    absolute = vorticity + coriolis.reshape(elements, 4, 4, 1)
    flux_one = geopot * veloc_one
    flux_two = geopot * veloc_two
    contra_one = (inv_aa * flux_one + inv_ab * flux_two) / jacobian_inv
    contra_two = (inv_ba * flux_one + inv_bb * flux_two) / jacobian_inv
    divergence = jacobian_inv * (
        along_cols(contra_one, derivative) + along_rows(contra_two, derivative)
    )
    tendency = jnp.stack(
        [absolute * veloc_two - grad_one, -absolute * veloc_one - grad_two, -divergence]
    )
    mass_weight = (weights[:, None] * weights[None, :])[None] / jacobian_inv[..., 0]
    return (tendency.reshape(3, elements, 16, levels), mass_weight.reshape(elements, 16))


def link_groups(lap_blocks):
    side_points = 3 * BY + 1
    top_points = 3 * BX + 1
    group_sizes = [
        (1, side_points),
        (-1, side_points),
        (lap_blocks, top_points),
        (-lap_blocks, top_points),
        (lap_blocks + 1, 1),
        (-lap_blocks - 1, 1),
        (lap_blocks - 1, 1),
        (1 - lap_blocks, 1),
    ]
    groups = []
    first_slot = 0
    for offset, slot_count in group_sizes:
        groups.append((offset, first_slot, slot_count))
        first_slot = first_slot + slot_count
    return groups


def select_table(indices, count):
    return (indices[:, None] == jnp.arange(count, dtype=jnp.int32)[None, :]).astype(jnp.bfloat16)


def split_dot(form, table, values):
    upper = values.astype(jnp.bfloat16)
    lower = (values - upper.astype(jnp.float32)).astype(jnp.bfloat16)
    first = jnp.einsum(form, table, upper, preferred_element_type=jnp.float32)
    return first + jnp.einsum(form, table, lower, preferred_element_type=jnp.float32)


def local(prognostic, metric, coriolis, node_point, send_point, recv_point):
    elements = prognostic.shape[1]
    levels = prognostic.shape[3]
    fields = prognostic.astype(jnp.float32)
    tendency, mass_weight = element_tendency(fields, metric, coriolis)
    point_ids = node_point.reshape(-1)
    weighted = (tendency * mass_weight[None, :, :, None]).reshape(3, elements * 16, levels)
    node_table = select_table(point_ids, PTS)
    partial_value = split_dot("np,fnl->fpl", node_table, weighted)
    weight = split_dot("np,n->p", node_table, mass_weight.reshape(-1))
    send_table = select_table(send_point, PTS)
    outgoing = split_dot("sp,fpl->fsl", send_table, partial_value)
    out_weight = split_dot("sp,p->s", send_table, weight)
    groups = link_groups(4 * lax.axis_size("sub"))

    def group_slice(values, masses, group_index):
        offset, first_slot, slot_count = groups[group_index]
        return (
            values[:, first_slot : first_slot + slot_count, :],
            masses[first_slot : first_slot + slot_count],
        )

    def split_bundle(bundle, members):
        result = {}
        cursor = 0
        for group_index in members:
            slot_count = groups[group_index][2]
            result[group_index] = (
                bundle[0][:, cursor : cursor + slot_count, :],
                bundle[1][cursor : cursor + slot_count],
            )
            cursor = cursor + slot_count
        return result

    arrived = [None] * 8
    lap_blocks = groups[2][0]
    landed_vertical = {}
    for direction, members in ((1, (2, 4, 6)), (-1, (3, 5, 7))):
        sections = [group_slice(outgoing, out_weight, group_index) for group_index in members]
        values_cat = jnp.concatenate([section[0] for section in sections], axis=1)
        masses_cat = jnp.concatenate([section[1] for section in sections], axis=0)
        landed = from_behind((values_cat, masses_cat), ("face", "sub"), direction * lap_blocks)
        landed_vertical[direction] = split_bundle(landed, members)
    from_below = landed_vertical[1]
    from_above = landed_vertical[-1]
    arrived[2] = from_below[2]
    arrived[3] = from_above[3]
    plans = (
        (1, (0, 4, 7), (group_slice(outgoing, out_weight, 0), from_below[4], from_above[7])),
        (-1, (1, 6, 5), (group_slice(outgoing, out_weight, 1), from_below[6], from_above[5])),
    )
    for direction, members, sections in plans:
        values_cat = jnp.concatenate([section[0] for section in sections], axis=1)
        masses_cat = jnp.concatenate([section[1] for section in sections], axis=0)
        landed = from_behind((values_cat, masses_cat), ("face", "sub"), direction)
        pieces_back = split_bundle(landed, members)
        for group_index in members:
            arrived[group_index] = pieces_back[group_index]
    received = jnp.concatenate([arrived[group_index][0] for group_index in range(8)], axis=1)
    received_weight = jnp.concatenate([arrived[group_index][1] for group_index in range(8)], axis=0)
    recv_table = select_table(recv_point, PTS)
    total = partial_value + split_dot("sp,fsl->fpl", recv_table, received)
    total_weight = weight + split_dot("sp,s->p", recv_table, received_weight)
    point_average = total / total_weight[None, :, None]
    averaged = split_dot("np,fpl->fnl", node_table, point_average)
    advanced = fields + STEP_SIZE * averaged.reshape(3, elements, 16, levels)
    return advanced.astype(jnp.bfloat16)


def solution(mesh):
    placed = (
        P(None, ("face", "sub"), None, None),
        P(None, ("face", "sub"), None),
        P(("face", "sub"), None),
        P(("face", "sub"), None),
        P(("face", "sub")),
        P(("face", "sub")),
    )
    return jax.shard_map(
        local,
        mesh=mesh,
        in_specs=placed,
        out_specs=P(None, ("face", "sub"), None, None),
        check_vma=False,
    )
```

profile of v0, /device:TPU:32, one launch (start us, length us, event | category | flops | bytes accessed | tf_op | source)
XLA Modules:
  0.0 113.9 jit_solution(7834143525173235909)
XLA Ops:
  0.9 1.2 %fusion.88 = (f32[1,64,16,128]{3,2,1,0:T(8,128)S(1)}, f32[1,64,16,128]{3,2,1,0:T(8,128)S(1)}, f32[1,64,16,128]{3,2,1,0:T(8,128)S(1)}) fusion(bf16[3,64,16,128]{3,2,1,0:T(8,128)(2,1)} %param.8), kind=kLoop, calls=%fused_computation.112 | loop fusion | bytes 3145728 | tf_op jit(solution)/shard_map/slice | solution.py:54
  5.1 1.8 %fusion.52 = f32[64,4,128,4]{2,3,1,0:T(4,128)} fusion(f32[4,4,1,1]{1,0,3,2:T(4,128)S(1)} %copy-done.5, f32[64,4,4,128]{3,2,1,0:T(4,128)S(1)} %get-tuple-element.13), kind=kOutput, calls=%fused_computation.56 | convolution fusion | flops 6291456 | bytes 1048640 | tf_op jit(solution)/shard_map/aj,ejcl->eacl/dot_general | solution.py:44
  11.3 1.6 %div.61 = f32[1024]{0:T(1024)} reshape(f32[64,4,4]{2,1,0:T(4,128)} %div.60) | data formatting | bytes 8192 | tf_op jit(solution)/shard_map/div | solution.py:82
  18.4 1.4 %div.58 = f32[1024]{0:T(1024)} reshape(f32[64,16]{1,0:T(8,128)} %div.57) | data formatting | bytes 8192 | tf_op jit(solution)/shard_map/div | solution.py:82
  19.8 3.8 %fusion.30 = f32[64,4,4,128]{3,2,1,0:T(4,128)S(1)} fusion(f32[4,4,1,1]{1,0,3,2:T(4,128)S(1)} %copy-done.5, f32[64,4,128,4]{2,3,1,0:T(4,128)} %fusion.52, f32[64,4,4]{2,1,0:T(4,128)} %copy.49, f32[64,4,4]{2,1,0:T(4,128)} %copy.48, f32[64,4,4]{2,1,0:T(4,128)S(1)} %copy.47, f32[64,4,4,128]{3,2,1,0:T(4,128)S(1)} %bitcast.120, ...), kind=kOutput, calls=%fused_computation.27 | convolution fusion | flops 7471104 | bytes 2633792 | tf_op jit(solution)/shard_map/aj,erjl->eral/dot_general | solution.py:40
  23.7 2.5 %fusion.33 = f32[64,4,4,128]{3,2,1,0:T(4,128)S(1)} fusion(f32[4,4,1,1]{1,0,3,2:T(4,128)S(1)} %copy-done.5, f32[64,4,128,4]{2,3,1,0:T(4,128)S(1)} %fusion.56, f32[64,4,4,128]{3,2,1,0:T(4,128)S(1)} %bitcast.113, f32[64,4,4,128]{3,2,1,0:T(4,128)S(1)} %bitcast.117, f32[64,4,4]{2,1,0:T(4,128)S(1)} %copy-done.3, f32[64,4,4]{2,1,0:T(4,128)S(1)} %copy-done.1, ...), kind=kOutput, calls=%fused_computation.31 | convolution fusion | flops 7208960 | bytes 2113600 | tf_op jit(solution)/shard_map/aj,erjl->eral/dot_general | solution.py:40
  26.2 2.1 %fusion.51 = (f32[64,4,4,128]{3,2,1,0:T(4,128)S(1)}, f32[64,4,4,128]{3,2,1,0:T(4,128)S(1)}) fusion(f32[64,4,4,128]{3,2,1,0:T(4,128)S(1)} %fusion.33, f32[64,4,4,128]{3,2,1,0:T(4,128)S(1)} %bitcast.118, f32[64,4,128,4]{2,3,1,0:T(4,128)S(1)} %fusion.54, f32[64,4,4]{2,1,0:T(4,128)S(1)} %copy-done.2, f32[64,4,4]{2,1,0:T(4,128)S(1)} %copy.51, ...), kind=kOutput, calls=%fused_computation.55 | convolution fusion | flops 7733248 | bytes 3686464 | tf_op jit(solution)/shard_map/aj,erjl->eral/dot_general | solution.py:40
  31.1 18.1 %collective-permute-start.1 = (f32[3,99,128]{2,1,0:T(8,128)S(1)}, f32[3,99,128]{2,1,0:T(8,128)S(1)}, u32[]{:S(2)}, u32[]{:S(2)}) collective-permute-start(f32[3,99,128]{2,1,0:T(8,128)S(1)} %pad_maximum_fusion.1), channel_id=1, source_target_pairs={{0,1008},{1,1009},{2,1010},{3,1011},{4,1012},{5,1013},{6,1014},{7,... | collective-permute-start | bytes 456200 | tf_op jit(solution)/shard_map/ppermute | solution.py:20
  49.3 1.9 %collective-permute-start = (f32[3,99,128]{2,1,0:T(8,128)S(1)}, f32[3,99,128]{2,1,0:T(8,128)S(1)}, u32[]{:S(2)}, u32[]{:S(2)}) collective-permute-start(f32[3,99,128]{2,1,0:T(8,128)S(1)} %pad_maximum_fusion), channel_id=1, source_target_pairs={{0,16},{1,17},{2,18},{3,19},{4,20},{5,21},{6,22},{7,23},{8,24},{9,... | collective-permute-start | bytes 456200 | tf_op jit(solution)/shard_map/ppermute | solution.py:20
  53.8 1.4 %pad_maximum_fusion.5 = f32[99]{0:T(128)S(1)} fusion(f32[1]{0:T(128)} %get-tuple-element.47, f32[1]{0:T(128)} %get-tuple-element.48, f32[97]{0:T(128)S(1)} %get-tuple-element.45), kind=kLoop, calls=%fused_computation.106 | loop fusion | flops 198 | bytes 792 | tf_op jit(solution)/shard_map/concatenate | solution.py:158
  55.2 8.1 %collective-permute-start.5 = (f32[99]{0:T(128)S(1)}, f32[99]{0:T(128)S(1)}, u32[]{:S(2)}, u32[]{:S(2)}) collective-permute-start(f32[99]{0:T(128)S(1)} %pad_maximum_fusion.5), channel_id=1, source_target_pairs={{0,1008},{1,1009},{2,1010},{3,1011},{4,1012},{5,1013},{6,1014},{7,... | collective-permute-start | bytes 1196 | tf_op jit(solution)/shard_map/ppermute | solution.py:20
  63.3 1.3 %pad_maximum_fusion.4 = f32[99]{0:T(128)S(1)} fusion(f32[1]{0:T(128)} %get-tuple-element.49, f32[1]{0:T(128)} %get-tuple-element.46, f32[97]{0:T(128)S(1)} %get-tuple-element.44), kind=kLoop, calls=%fused_computation.105 | loop fusion | flops 198 | bytes 792 | tf_op jit(solution)/shard_map/concatenate | solution.py:158
  64.6 1.9 %collective-permute-start.4 = (f32[99]{0:T(128)S(1)}, f32[99]{0:T(128)S(1)}, u32[]{:S(2)}, u32[]{:S(2)}) collective-permute-start(f32[99]{0:T(128)S(1)} %pad_maximum_fusion.4), channel_id=1, source_target_pairs={{0,16},{1,17},{2,18},{3,19},{4,20},{5,21},{6,22},{7,23},{8,24},{9,... | collective-permute-start | bytes 1196 | tf_op jit(solution)/shard_map/ppermute | solution.py:20
  67.3 7.0 %collective-permute-done.4 = f32[99]{0:T(128)S(1)} collective-permute-done((f32[99]{0:T(128)S(1)}, f32[99]{0:T(128)S(1)}, u32[]{:S(2)}, u32[]{:S(2)}) %collective-permute-start.4) | collective-permute-done | bytes 428 | tf_op jit(solution)/shard_map/ppermute | solution.py:20
  74.9 1.4 %pad_maximum_fusion.6 = f32[9]{0:T(128)S(1)} fusion(f32[1]{0:T(128)} %get-tuple-element.57, f32[1]{0:T(128)} %get-tuple-element.55, f32[7]{0:T(128)S(1)} %get-tuple-element.43), kind=kLoop, calls=%fused_computation.107 | loop fusion | flops 18 | bytes 72 | tf_op jit(solution)/shard_map/concatenate | solution.py:171
  76.3 3.4 %collective-permute-start.6 = (f32[9]{0:T(128)S(1)}, f32[9]{0:T(128)S(1)}, u32[]{:S(2)}, u32[]{:S(2)}) collective-permute-start(f32[9]{0:T(128)S(1)} %pad_maximum_fusion.6), channel_id=1, source_target_pairs={{0,1},{1,2},{2,3},{3,4},{4,5},{5,6},{6,7},{7,8},{8,9},{9,10},{10,1... | collective-permute-start | bytes 116 | tf_op jit(solution)/shard_map/ppermute | solution.py:20
  79.7 1.4 %pad_maximum_fusion.7 = f32[9]{0:T(128)S(1)} fusion(f32[1]{0:T(128)} %get-tuple-element.56, f32[1]{0:T(128)} %get-tuple-element.54, f32[7]{0:T(128)S(1)} %get-tuple-element.42), kind=kLoop, calls=%fused_computation.108 | loop fusion | flops 18 | bytes 72 | tf_op jit(solution)/shard_map/concatenate | solution.py:171
  81.0 7.6 %collective-permute-start.7 = (f32[9]{0:T(128)S(1)}, f32[9]{0:T(128)S(1)}, u32[]{:S(2)}, u32[]{:S(2)}) collective-permute-start(f32[9]{0:T(128)S(1)} %pad_maximum_fusion.7), channel_id=1, source_target_pairs={{0,1023},{1,0},{2,1},{3,2},{4,3},{5,4},{6,5},{7,6},{8,7},{9,8},{10... | collective-permute-start | bytes 116 | tf_op jit(solution)/shard_map/ppermute | solution.py:20
  90.5 2.7 %concatenate.41 = f32[212]{0:T(256)S(1)} concatenate(f32[7]{0:T(128)S(1)} %bitcast.135, f32[7]{0:T(128)S(1)} %bitcast.136, f32[97]{0:T(128)S(1)} %bitcast.134, f32[97]{0:T(128)S(1)} %bitcast.133, f32[1]{0:T(128)} %get-tuple-element.51, f32[1]{0:T(128)} %get-tuple-element.53, f32[1]{0:T(128)} %get-tuple-element.52, f32[1]{0:T(128)} %get-tuple-element.50), dimensions={0} | concatenate | bytes 1696 | tf_op jit(solution)/shard_map/concatenate | solution.py:177
  93.9 1.9 %collective-permute-start.2 = (f32[3,9,128]{2,1,0:T(8,128)S(1)}, f32[3,9,128]{2,1,0:T(8,128)S(1)}, u32[]{:S(2)}, u32[]{:S(2)}) collective-permute-start(f32[3,9,128]{2,1,0:T(8,128)S(1)} %pad_maximum_fusion.2), channel_id=1, source_target_pairs={{0,1},{1,2},{2,3},{3,4},{4,5},{5,6},{6,7},{7,8},{8,9},{9,10},{10,1... | collective-permute-start | bytes 41480 | tf_op jit(solution)/shard_map/ppermute | solution.py:20
  95.8 9.3 %collective-permute-start.3 = (f32[3,9,128]{2,1,0:T(8,128)S(1)}, f32[3,9,128]{2,1,0:T(8,128)S(1)}, u32[]{:S(2)}, u32[]{:S(2)}) collective-permute-start(f32[3,9,128]{2,1,0:T(8,128)S(1)} %pad_maximum_fusion.3), channel_id=1, source_target_pairs={{0,1023},{1,0},{2,1},{3,2},{4,3},{5,4},{6,5},{7,6},{8,7},{9,8},{10... | collective-permute-start | bytes 41480 | tf_op jit(solution)/shard_map/ppermute | solution.py:20
  105.1 1.3 %collective-permute-done.3 = f32[3,9,128]{2,1,0:T(8,128)S(1)} collective-permute-done((f32[3,9,128]{2,1,0:T(8,128)S(1)}, f32[3,9,128]{2,1,0:T(8,128)S(1)}, u32[]{:S(2)}, u32[]{:S(2)}) %collective-permute-start.3) | collective-permute-done | bytes 13856 | tf_op jit(solution)/shard_map/ppermute | solution.py:20
  108.9 2.1 %multiply_bitcast_fusion = f32[3,1024,128]{1,2,0:T(8,128)} fusion(f32[3,128,1024]{2,1,0:T(8,128)S(1)} %fusion.3, s32[1024]{0:T(1024)S(1)} %eq.20, f32[3,679,128]{2,1,0:T(8,128)S(1)} %fusion.27), kind=kOutput, calls=%fused_computation.10 | convolution fusion | flops 535729792 | bytes 4192768 | tf_op jit(solution)/shard_map/np,fpl->fnl/dot_general | solution.py:114
  110.9 1.9 %copy.63 = f32[3,1024,128]{2,1,0:T(8,128)S(1)} copy(f32[3,1024,128]{1,2,0:T(8,128)} %multiply_bitcast_fusion) | data formatting | bytes 3145728 | tf_op jit(solution)/shard_map/mul | solution.py:183
  (97 shorter events, 26.3 us)
Async XLA Ops:
  0.9 1.3 %copy-start.4 = (f32[4,64,16]{1,2,0:T(8,128)S(1)}, f32[4,64,16]{1,2,0:T(8,128)}, u32[]{:S(2)}) copy-start(f32[4,64,16]{1,2,0:T(8,128)} %param.9) | copy-start | bytes 49156
  4.1 1.0 copy-start.5
  5.1 2.9 %copy-start.8 = (f32[64,16]{0,1:T(8,128)S(1)}, f32[64,16]{0,1:T(8,128)}, u32[]{:S(2)}) copy-start(f32[64,16]{0,1:T(8,128)} %param.10) | copy-start | bytes 12292
  19.8 3.8 %copy-start.1 = (f32[64,4,4]{2,1,0:T(4,128)S(1)}, f32[64,4,4]{2,1,0:T(4,128)}, u32[]{:S(2)}) copy-start(f32[64,4,4]{2,1,0:T(4,128)} %copy.49) | copy-start | bytes 12292
  19.8 3.9 %copy-start.2 = (f32[64,4,4]{2,1,0:T(4,128)S(1)}, f32[64,4,4]{2,1,0:T(4,128)}, u32[]{:S(2)}) copy-start(f32[64,4,4]{2,1,0:T(4,128)} %copy.48) | copy-start | bytes 12292
  19.8 3.9 %copy-start.3 = (f32[64,4,4]{2,1,0:T(4,128)S(1)}, f32[64,4,4]{2,1,0:T(4,128)}, u32[]{:S(2)}) copy-start(f32[64,4,4]{2,1,0:T(4,128)} %copy.54) | copy-start | bytes 12292
  26.2 2.1 %copy-start.6 = (f32[1024]{0:T(1024)S(1)}, f32[1024]{0:T(1024)}, u32[]{:S(2)}) copy-start(f32[1024]{0:T(1024)} %div.61) | copy-start | bytes 12292
  26.2 2.1 %copy-start.7 = (f32[1024]{0:T(1024)S(1)}, f32[1024]{0:T(1024)}, u32[]{:S(2)}) copy-start(f32[1024]{0:T(1024)} %div.58) | copy-start | bytes 12292
  29.2 1.0 copy-start.9
  31.1 62.2 %copy-start.10 = (s32[212]{0:T(256)S(1)}, s32[212]{0:T(256)}, u32[]{:S(2)}) copy-start(s32[212]{0:T(256)} %param.13) | copy-start | bytes 2548
  31.1 62.7 %collective-permute-start.1 = (f32[3,99,128]{2,1,0:T(8,128)S(1)}, f32[3,99,128]{2,1,0:T(8,128)S(1)}, u32[]{:S(2)}, u32[]{:S(2)}) collective-permute-start(f32[3,99,128]{2,1,0:T(8,128)S(1)} %pad_maximum_fusion.1), channel_id=1, source_target_pairs={{0,1008},{1,1009},{2,1010},{3,1011},{4,1012},{5,1013},{6,1014},{7,... | collective-permute-start | bytes 456200 | tf_op jit(solution)/shard_map/ppermute | solution.py:20
  49.3 44.6 %collective-permute-start = (f32[3,99,128]{2,1,0:T(8,128)S(1)}, f32[3,99,128]{2,1,0:T(8,128)S(1)}, u32[]{:S(2)}, u32[]{:S(2)}) collective-permute-start(f32[3,99,128]{2,1,0:T(8,128)S(1)} %pad_maximum_fusion), channel_id=1, source_target_pairs={{0,16},{1,17},{2,18},{3,19},{4,20},{5,21},{6,22},{7,23},{8,24},{9,... | collective-permute-start | bytes 456200 | tf_op jit(solution)/shard_map/ppermute | solution.py:20
  55.2 11.5 %collective-permute-start.5 = (f32[99]{0:T(128)S(1)}, f32[99]{0:T(128)S(1)}, u32[]{:S(2)}, u32[]{:S(2)}) collective-permute-start(f32[99]{0:T(128)S(1)} %pad_maximum_fusion.5), channel_id=1, source_target_pairs={{0,1008},{1,1009},{2,1010},{3,1011},{4,1012},{5,1013},{6,1014},{7,... | collective-permute-start | bytes 1196 | tf_op jit(solution)/shard_map/ppermute | solution.py:20
  64.6 9.7 %collective-permute-start.4 = (f32[99]{0:T(128)S(1)}, f32[99]{0:T(128)S(1)}, u32[]{:S(2)}, u32[]{:S(2)}) collective-permute-start(f32[99]{0:T(128)S(1)} %pad_maximum_fusion.4), channel_id=1, source_target_pairs={{0,16},{1,17},{2,18},{3,19},{4,20},{5,21},{6,22},{7,23},{8,24},{9,... | collective-permute-start | bytes 1196 | tf_op jit(solution)/shard_map/ppermute | solution.py:20
  76.3 12.3 %collective-permute-start.6 = (f32[9]{0:T(128)S(1)}, f32[9]{0:T(128)S(1)}, u32[]{:S(2)}, u32[]{:S(2)}) collective-permute-start(f32[9]{0:T(128)S(1)} %pad_maximum_fusion.6), channel_id=1, source_target_pairs={{0,1},{1,2},{2,3},{3,4},{4,5},{5,6},{6,7},{7,8},{8,9},{9,10},{10,1... | collective-permute-start | bytes 116 | tf_op jit(solution)/shard_map/ppermute | solution.py:20
  81.0 8.9 %collective-permute-start.7 = (f32[9]{0:T(128)S(1)}, f32[9]{0:T(128)S(1)}, u32[]{:S(2)}, u32[]{:S(2)}) collective-permute-start(f32[9]{0:T(128)S(1)} %pad_maximum_fusion.7), channel_id=1, source_target_pairs={{0,1023},{1,0},{2,1},{3,2},{4,3},{5,4},{6,5},{7,6},{8,7},{9,8},{10... | collective-permute-start | bytes 116 | tf_op jit(solution)/shard_map/ppermute | solution.py:20
  93.9 11.2 %collective-permute-start.2 = (f32[3,9,128]{2,1,0:T(8,128)S(1)}, f32[3,9,128]{2,1,0:T(8,128)S(1)}, u32[]{:S(2)}, u32[]{:S(2)}) collective-permute-start(f32[3,9,128]{2,1,0:T(8,128)S(1)} %pad_maximum_fusion.2), channel_id=1, source_target_pairs={{0,1},{1,2},{2,3},{3,4},{4,5},{5,6},{6,7},{7,8},{8,9},{9,10},{10,1... | collective-permute-start | bytes 41480 | tf_op jit(solution)/shard_map/ppermute | solution.py:20
  95.8 10.6 %collective-permute-start.3 = (f32[3,9,128]{2,1,0:T(8,128)S(1)}, f32[3,9,128]{2,1,0:T(8,128)S(1)}, u32[]{:S(2)}, u32[]{:S(2)}) collective-permute-start(f32[3,9,128]{2,1,0:T(8,128)S(1)} %pad_maximum_fusion.3), channel_id=1, source_target_pairs={{0,1023},{1,0},{2,1},{3,2},{4,3},{5,4},{6,5},{7,6},{8,7},{9,8},{10... | collective-permute-start | bytes 41480 | tf_op jit(solution)/shard_map/ppermute | solution.py:20
  110.9 2.0 %copy-start = (bf16[3,64,16,128]{3,2,1,0:T(8,128)(2,1)S(1)}, bf16[3,64,16,128]{3,2,1,0:T(8,128)(2,1)}, u32[]{:S(2)}) copy-start(bf16[3,64,16,128]{3,2,1,0:T(8,128)(2,1)} %param.8) | copy-start | bytes 2359300
where the time goes:
time: 115 us; the launch traced here: 114 us
  starting transfers between devices  52.2 us (45%)
  local copies, waits for them, and re-layouts  22 us (19%)
  matrix products  21.2 us (18%)
  other arithmetic  9.04 us (8%)
  waiting for transfers between devices  8.89 us (8%)
    ppermute x8, starting transfers between devices, from_behind(): return lax.ppermute(value, axis, pairs)  52.2 us
    ppermute x8, waiting for transfers between devices, from_behind(): return lax.ppermute(value, axis, pairs)  8.89 us
    dot_general x3, matrix products, along_cols(): jnp.einsum('aj,erjl->eral', derivative, values, precision=lax.Precision.H...  8.39 us
    concatenate x4, other arithmetic, local(): masses_cat = jnp.concatenate([section[1] for section in sections], axis=0)  5.45 us
    dot_general x7, matrix products, split_dot(): first = jnp.einsum(form, table, upper, preferred_element_type=jnp.float32)  5.07 us
    div x4, local copies, waits for them, and re-layouts, element_tendency(): (weights[:, None] * weights[None, :])[None] / jacobian_inv[..., 0]  4.35 us
    dot_general x7, matrix products, split_dot(): jnp.einsum(form, table, lower, preferred_element_type=jnp.float32)  3.89 us
    dot_general x3, matrix products, along_rows(): jnp.einsum('aj,ejcl->eacl', derivative, values, precision=lax.Precision.H...  3.87 us
  transfers between devices with their start and end apart: 8, of which 3 were waited for; matrix products, arithmetic and copies ran while one was open for 12% of the time, Pallas kernels for 0%

commit v1 on v0

v1 whole, which is shorter than its diff:
```python
import functools
import math

import jax
import jax.numpy as jnp
import numpy as np
from jax import lax
from jax.experimental import pallas as pl
from jax.experimental.pallas import tpu as pltpu
from jax.sharding import PartitionSpec as P

MESH = pl.DeviceIdType.MESH
BX = 32
BY = 2
ELEMS = BX * BY
NODES = ELEMS * 16
LEV = 128
SIDE = 3 * BY + 1
TOP = 3 * BX + 1
LINKS = 2 * SIDE + 2 * TOP + 4
STEP_SIZE = 0.1
BLK = 16

GROUPS = (
    (2, 2 * SIDE, TOP, 0, 104),
    (3, 2 * SIDE + TOP, TOP, 128, 104),
    (0, 0, SIDE, 104, 8),
    (1, SIDE, SIDE, 232, 8),
    (4, 2 * SIDE + 2 * TOP, 1, 112, 8),
    (5, 2 * SIDE + 2 * TOP + 1, 1, 240, 8),
    (6, 2 * SIDE + 2 * TOP + 2, 1, 120, 8),
    (7, 2 * SIDE + 2 * TOP + 3, 1, 248, 8),
)
ROWS = 256


def gll_tables():
    abscissa = np.array([-1.0, -math.sqrt(0.2), math.sqrt(0.2), 1.0])
    legendre = 0.5 * (5.0 * abscissa * abscissa * abscissa - 3.0 * abscissa)
    derivative = np.zeros((4, 4))
    for target in range(4):
        for source in range(4):
            if target != source:
                derivative[target, source] = legendre[target] / (
                    legendre[source] * (abscissa[target] - abscissa[source])
                )
    derivative[0, 0] = -3.0
    derivative[3, 3] = 3.0
    weights = np.array([1.0, 5.0, 5.0, 1.0]) / 6.0
    return derivative, weights


DERIV, GLL = gll_tables()
EV0 = float(0.5 * (DERIV[0, 0] + DERIV[0, 3]))
EV1 = float(0.5 * (DERIV[1, 0] + DERIV[1, 3]))
OD00 = float(0.5 * (DERIV[0, 0] - DERIV[0, 3]))
OD01 = float(0.5 * (DERIV[0, 1] - DERIV[0, 2]))
OD10 = float(0.5 * (DERIV[1, 0] - DERIV[1, 3]))
OD11 = float(0.5 * (DERIV[1, 1] - DERIV[1, 2]))


def derive4(s):
    o0 = s[0] - s[3]
    o1 = s[1] - s[2]
    q = (s[0] + s[3]) - (s[1] + s[2])
    h0 = OD00 * o0 + OD01 * o1
    h1 = OD10 * o0 + OD11 * o1
    g0 = EV0 * q
    g1 = EV1 * q
    return [h0 + g0, h1 + g1, h1 - g1, h0 - g0]


def along_cols(s):
    out = []
    for r in range(4):
        out += derive4(s[4 * r : 4 * r + 4])
    return out


def along_rows(s):
    out = [None] * 16
    for c in range(4):
        for r, value in enumerate(derive4(s[c::4])):
            out[4 * r + c] = value
    return out


NODE_W = [float(GLL[n // 4] * GLL[n % 4]) for n in range(16)]


def lane_iota(shape):
    return lax.broadcasted_iota(jnp.int32, shape, len(shape) - 1)


def padded_slots(ref):
    x = jnp.concatenate(
        [jnp.broadcast_to(ref[...], (8, LINKS)), jnp.full((8, ROWS - LINKS), -1, jnp.int32)], axis=1
    )
    lane = lane_iota((8, ROWS))
    out = jnp.full((8, ROWS), -1, jnp.int32)
    for _, first, count, row, _ in GROUPS:
        moved = pltpu.roll(x, (row - first) % ROWS, 1)
        out = jnp.where((lane >= row) & (lane < row + count), moved, out)
    return out


def one_hot(col, row):
    return jnp.where(col == row, 1.0, 0.0).astype(jnp.bfloat16)


def kernel(
    sizes,
    prog_hbm, met_hbm, cor_hbm, np_hbm, sp_hbm, rp_hbm,
    out_ref,
    prog_v, met_v, cor_v, np_v, sp_v, rp_v,
    f_v, ct_v, w_v, s_v, a_v, r_v, acc_v, inv_v, ids_v, out_b, in_b,
    in_sem, send_sem, recv_sem,
):
    n_face, n_sub = sizes
    total = n_face * n_sub
    lap = 4 * n_sub
    offsets = (1, -1, lap, -lap, lap + 1, -lap - 1, lap - 1, 1 - lap)
    me = lax.axis_index("face") * n_sub + lax.axis_index("sub")

    def device(offset):
        t = lax.rem(me + (offset + total), total)
        return (t // n_sub, lax.rem(t, n_sub))

    loads = []
    for i, (src, dst) in enumerate(
        ((np_hbm, np_v), (sp_hbm, sp_v), (rp_hbm, rp_v), (met_hbm, met_v), (cor_hbm, cor_v))
    ):
        loads.append(pltpu.make_async_copy(src, dst, in_sem.at[i]))
    for f in range(3):
        loads.append(pltpu.make_async_copy(prog_hbm.at[f], prog_v.at[f], in_sem.at[5 + f]))
    for load in loads:
        load.start()

    barrier = pltpu.get_barrier_semaphore()
    for offset in offsets:
        pl.semaphore_signal(barrier, inc=1, device_id=device(offset), device_id_type=MESH)

    def remote(f, g):
        group, _, _, row, rows = g
        return pltpu.make_async_remote_copy(
            src_ref=out_b.at[f, pl.ds(row, rows)],
            dst_ref=in_b.at[f, pl.ds(row, rows)],
            send_sem=send_sem.at[f, group],
            recv_sem=recv_sem.at[f, group],
            device_id=device(offsets[group]),
            device_id_type=MESH,
        )

    for load in loads[:3]:
        load.wait()
    ids = np_v[...]
    ids2 = jnp.concatenate([ids, ids], axis=1)
    ids_v[...] = ids2
    half = lane_iota((8, LEV)) < ELEMS
    id_rows = []
    for j in range(8):
        even = jnp.broadcast_to(ids2[2 * j : 2 * j + 1], (8, LEV))
        odd = jnp.broadcast_to(ids2[2 * j + 1 : 2 * j + 2], (8, LEV))
        id_rows.append(jnp.where(half, even, odd)[0:1])
    send_row = padded_slots(sp_v)
    recv_row = padded_slots(rp_v)
    for chunk in range(2):
        col = jnp.transpose(
            jnp.broadcast_to(send_row[0:1, 128 * chunk : 128 * chunk + 128], (128, 128))
        )
        for j in range(8):
            s_v[128 * chunk : 128 * chunk + 128, 128 * j : 128 * j + 128] = one_hot(col, id_rows[j])

    for load in loads[3:5]:
        load.wait()
    m_a, m_b, m_e, m_g = (met_v[i] for i in range(4))
    inverse = 1.0 / (m_a * m_g - m_b * m_e)
    node = lax.broadcasted_iota(jnp.int32, (16, ELEMS), 0)
    wr = jnp.where((node < 4) | (node >= 12), float(GLL[0]), float(GLL[1]))
    wc = jnp.where((node % 4 == 0) | (node % 4 == 3), float(GLL[0]), float(GLL[1]))
    mass = wr * wc * inverse
    coefs = jnp.concatenate(
        [m_a * inverse, m_b * inverse, m_e * inverse, m_g * inverse, mass * cor_v[...], mass, mass, mass],
        axis=0,
    )
    ct_v[...] = jnp.transpose(coefs)

    for f in range(3):
        loads[5 + f].wait()
        f_v[NODES * f : NODES * f + NODES] = prog_v[f].astype(jnp.float32)

    def fields_of(k):
        base = k * (BLK * 16)
        return [
            [f_v[pl.ds(f * NODES + base + n, BLK, stride=16), :] for n in range(16)]
            for f in range(3)
        ]

    def spread(ct, q, n):
        i = q * 16 + n
        return jnp.broadcast_to(ct[:, i : i + 1], (BLK, LEV))

    def rows_of(k, n):
        return pl.ds(pl.multiple_of(n * ELEMS + k * BLK, BLK), BLK)

    def first_pass(k, carry):
        u1, u2, phi = fields_of(k)
        ct = ct_v[pl.ds(pl.multiple_of(k * BLK, BLK), BLK), :]
        con1, con2 = [], []
        low = lane_iota((BLK, LEV)) < 64
        for n in range(16):
            f1 = phi[n] * u1[n]
            f2 = phi[n] * u2[n]
            con1.append(spread(ct, 0, n) * f1 + spread(ct, 1, n) * f2)
            con2.append(spread(ct, 2, n) * f1 + spread(ct, 3, n) * f2)
            mass = spread(ct, 5, n)
            high = mass.astype(jnp.bfloat16).astype(jnp.float32)
            w_v[rows_of(k, n), 128:256] = jnp.where(low, high, mass - high).astype(jnp.bfloat16)
        d1 = along_cols(con1)
        d2 = along_rows(con2)
        for n in range(16):
            w_v[rows_of(k, n), 0:128] = (-NODE_W[n] * (d1[n] + d2[n])).astype(jnp.bfloat16)
        return carry

    lax.fori_loop(0, ELEMS // BLK, first_pass, 0)

    sent = jnp.dot(s_v[...], w_v[:, 0:256], preferred_element_type=jnp.float32)
    out_b[0] = sent[:, 0:128]
    weight = sent[:, 128:256]
    weight = weight + pltpu.roll(weight, 64, 1)
    diagonal = lax.broadcasted_iota(jnp.int32, (128, 128), 0) == lane_iota((128, 128))
    for chunk in range(2):
        row = jnp.sum(
            jnp.where(diagonal, weight[128 * chunk : 128 * chunk + 128], 0.0), axis=0, keepdims=True
        )
        for _, _, count, first, _ in GROUPS:
            if first // 128 == chunk:
                out_b[0, first + count : first + count + 1, :] = row
    pl.semaphore_wait(barrier, len(offsets))
    for g in GROUPS:
        remote(0, g).start()

    def second_pass(k, carry):
        u1, u2, phi = fields_of(k)
        ct = ct_v[pl.ds(pl.multiple_of(k * BLK, BLK), BLK), :]
        energy, cov1, cov2 = [], [], []
        for n in range(16):
            energy.append(0.5 * (u1[n] * u1[n] + u2[n] * u2[n]) + phi[n])
            cov1.append(spread(ct, 3, n) * u1[n] - spread(ct, 2, n) * u2[n])
            cov2.append(spread(ct, 0, n) * u2[n] - spread(ct, 1, n) * u1[n])
        curl1 = along_cols(cov2)
        curl2 = along_rows(cov1)
        e1 = along_cols(energy)
        e2 = along_rows(energy)
        for n in range(16):
            eta = NODE_W[n] * (curl1[n] - curl2[n]) + spread(ct, 4, n)
            grad1 = spread(ct, 0, n) * e1[n] + spread(ct, 2, n) * e2[n]
            grad2 = spread(ct, 1, n) * e1[n] + spread(ct, 3, n) * e2[n]
            w_v[rows_of(k, n), 256:384] = (eta * u2[n] - NODE_W[n] * grad1).astype(jnp.bfloat16)
            w_v[rows_of(k, n), 384:512] = (-eta * u1[n] - NODE_W[n] * grad2).astype(jnp.bfloat16)
        return carry

    lax.fori_loop(0, ELEMS // BLK, second_pass, 0)
    sent = jnp.dot(s_v[...], w_v[:, 256:512], preferred_element_type=jnp.float32)
    for f in (1, 2):
        out_b[f] = sent[:, 128 * (f - 1) : 128 * f]
        for g in GROUPS:
            remote(f, g).start()

    def table(e, carry):
        x = ids_v[...]
        col = jnp.broadcast_to(pltpu.roll(x, LEV - e, 1)[:, 0:1], (16, LEV))
        rows = pl.ds(pl.multiple_of(e * 16, 16), 16)
        for j in range(8):
            a_v[rows, 128 * j : 128 * j + 128] = one_hot(col, id_rows[j])
        for chunk in range(2):
            r_v[rows, 128 * chunk : 128 * chunk + 128] = one_hot(
                col, recv_row[0:1, 128 * chunk : 128 * chunk + 128]
            )
        return carry

    lax.fori_loop(0, ELEMS, table, 0)

    def gather(i, carry):
        rows = pl.ds(pl.multiple_of(i * 256, 256), 256)
        acc_v[rows, :] = jnp.dot(a_v[rows, :], w_v[...], preferred_element_type=jnp.float32)
        return carry

    lax.fori_loop(0, NODES // 256, gather, 0)

    def finish(f, cols):
        def body(i, carry):
            rows = pl.ds(pl.multiple_of(i * 256, 256), 256)
            got = jnp.dot(
                r_v[rows, :], in_b[f].astype(jnp.bfloat16), preferred_element_type=jnp.float32
            )
            got = got + acc_v[rows, cols : cols + 128]
            field = prog_v[(f + 2) % 3, rows, :].astype(jnp.float32)
            out_ref[(f + 2) % 3, rows, :] = (field + got * inv_v[rows, :]).astype(jnp.bfloat16)
            return carry

        lax.fori_loop(0, NODES // 256, body, 0)

    for g in GROUPS:
        remote(0, g).wait_recv()
    lane = lane_iota((1, 128))
    low = lane_iota((128, 128)) < 64
    blocks = []
    for chunk in range(2):
        row = jnp.zeros((1, 128), jnp.float32)
        for _, _, count, first, _ in GROUPS:
            if first // 128 == chunk:
                at = first % 128
                row = jnp.where(
                    (lane >= at) & (lane < at + count), in_b[0, first + count : first + count + 1, :], row
                )
        col = jnp.transpose(jnp.broadcast_to(row, (128, 128)))
        high = col.astype(jnp.bfloat16).astype(jnp.float32)
        blocks.append(jnp.where(low, high, col - high).astype(jnp.bfloat16))
    arrived = jnp.concatenate(blocks, axis=0)

    def weights(i, carry):
        rows = pl.ds(pl.multiple_of(i * 256, 256), 256)
        w = jnp.dot(r_v[rows, :], arrived, preferred_element_type=jnp.float32)
        w = w + acc_v[rows, 128:256]
        w = w + pltpu.roll(w, 64, 1)
        inv_v[rows, :] = STEP_SIZE / w
        return carry

    lax.fori_loop(0, NODES // 256, weights, 0)
    finish(0, 0)
    for f in (1, 2):
        for g in GROUPS:
            remote(f, g).wait_recv()
        finish(f, 128 + 128 * f)
    for f in range(3):
        for g in GROUPS:
            remote(f, g).wait_send()


def solution(mesh):
    sizes = (mesh.shape["face"], mesh.shape["sub"])

    def local(prognostic, metric, coriolis, node_point, send_point, recv_point):
        result = pl.pallas_call(
            functools.partial(kernel, sizes),
            out_shape=jax.ShapeDtypeStruct((3, NODES, LEV), jnp.bfloat16),
            in_specs=[pl.BlockSpec(memory_space=pl.ANY)] * 6,
            out_specs=pl.BlockSpec(memory_space=pltpu.VMEM),
            scratch_shapes=[
                pltpu.VMEM((3, NODES, LEV), jnp.bfloat16),
                pltpu.VMEM((4, 16, ELEMS), jnp.float32),
                pltpu.VMEM((16, ELEMS), jnp.float32),
                pltpu.VMEM((16, ELEMS), jnp.int32),
                pltpu.VMEM((1, LINKS), jnp.int32),
                pltpu.VMEM((1, LINKS), jnp.int32),
                pltpu.VMEM((3 * NODES, LEV), jnp.float32),
                pltpu.VMEM((ELEMS, 128), jnp.float32),
                pltpu.VMEM((NODES, 512), jnp.bfloat16),
                pltpu.VMEM((ROWS, NODES), jnp.bfloat16),
                pltpu.VMEM((NODES, NODES), jnp.bfloat16),
                pltpu.VMEM((NODES, ROWS), jnp.bfloat16),
                pltpu.VMEM((NODES, 512), jnp.float32),
                pltpu.VMEM((NODES, LEV), jnp.float32),
                pltpu.VMEM((16, LEV), jnp.int32),
                pltpu.VMEM((3, ROWS, LEV), jnp.float32),
                pltpu.VMEM((3, ROWS, LEV), jnp.float32),
                pltpu.SemaphoreType.DMA((8,)),
                pltpu.SemaphoreType.DMA((3, 8)),
                pltpu.SemaphoreType.DMA((3, 8)),
            ],
            compiler_params=pltpu.CompilerParams(collective_id=0, has_side_effects=True),
        )(
            prognostic.reshape(3, NODES, LEV),
            jnp.transpose(metric, (0, 2, 1)),
            jnp.transpose(coriolis),
            jnp.transpose(node_point),
            send_point.reshape(1, LINKS),
            recv_point.reshape(1, LINKS),
        )
        return result.reshape(3, ELEMS, 16, LEV)

    placed = (
        P(None, ("face", "sub"), None, None),
        P(None, ("face", "sub"), None),
        P(("face", "sub"), None),
        P(("face", "sub"), None),
        P(("face", "sub")),
        P(("face", "sub")),
    )
    return jax.shard_map(
        local,
        mesh=mesh,
        in_specs=placed,
        out_specs=P(None, ("face", "sub"), None, None),
        check_vma=False,
    )
```

time: 115 us -> 43.5 us (0.38)
  the two profiles are of different devices: /device:TPU:32 before, /device:TPU:1 now
where the time goes in v1:
time: 43.5 us; the launch traced here: 43.3 us
  Pallas kernels  41.1 us (94%)
  local copies, waits for them, and re-layouts  2.15 us (5%)
    pallas_call x1, Pallas kernels, local(): pl.pallas_call(functools.partial(kernel, sizes), out_shape=jax.ShapeDtype...  41.1 us
    unnamed x1, local copies, waits for them, and re-layouts  2.15 us

profile of v1, /device:TPU:1, one launch (start us, length us, event | category | flops | bytes accessed | tf_op | source)
XLA Modules:
  0.0 43.3 jit_solution(10188944904224696300)
XLA Ops:
  0.0 41.1 %shard_map.64 = bf16[3,1024,128]{2,1,0:T(8,128)(2,1)} custom-call(bf16[3,1024,128]{2,1,0:T(8,128)(2,1)} %bitcast.8, f32[4,16,64]{2,1,0:T(8,128)} %bitcast.9, f32[16,64]{1,0:T(8,128)} %bitcast.10, s32[16,64]{1,0:T(8,128)} %bitcast.11, s32[1,212]{1,0:T(1,128)} %bitcast.12, s32[1,212]{1,0:T(1,128)} %bitcast.13), custom_call_target="tpu_custom_call" | custom-call | tf_op jit(solution)/shard_map/pallas_call | solution.py:345
  41.1 2.1 %copy.8 = bf16[3,64,16,128]{3,2,1,0:T(8,128)(2,1)} copy(bf16[3,64,16,128]{3,2,1,0:T(8,128)(2,1)} %bitcast.7) | data formatting | bytes 1572864

commit v2 on v1

--- a/solution.py
+++ b/solution.py
@@ -20,16 +20,18 @@
 LINKS = 2 * SIDE + 2 * TOP + 4
 STEP_SIZE = 0.1
 BLK = 16
+BLOCKS = ELEMS // BLK
+BROWS = 16 * BLK
 
 GROUPS = (
-    (2, 2 * SIDE, TOP, 0, 104),
-    (3, 2 * SIDE + TOP, TOP, 128, 104),
-    (0, 0, SIDE, 104, 8),
-    (1, SIDE, SIDE, 232, 8),
-    (4, 2 * SIDE + 2 * TOP, 1, 112, 8),
-    (5, 2 * SIDE + 2 * TOP + 1, 1, 240, 8),
-    (6, 2 * SIDE + 2 * TOP + 2, 1, 120, 8),
-    (7, 2 * SIDE + 2 * TOP + 3, 1, 248, 8),
+    (2, 2 * SIDE, TOP, 0),
+    (3, 2 * SIDE + TOP, TOP, 128),
+    (0, 0, SIDE, 104),
+    (1, SIDE, SIDE, 232),
+    (4, 2 * SIDE + 2 * TOP, 1, 112),
+    (5, 2 * SIDE + 2 * TOP + 1, 1, 240),
+    (6, 2 * SIDE + 2 * TOP + 2, 1, 120),
+    (7, 2 * SIDE + 2 * TOP + 3, 1, 248),
 )
 ROWS = 256
 
@@ -98,7 +100,7 @@
     )
     lane = lane_iota((8, ROWS))
     out = jnp.full((8, ROWS), -1, jnp.int32)
-    for _, first, count, row, _ in GROUPS:
+    for _, first, count, row in GROUPS:
         moved = pltpu.roll(x, (row - first) % ROWS, 1)
         out = jnp.where((lane >= row) & (lane < row + count), moved, out)
     return out
@@ -113,7 +115,7 @@
     prog_hbm, met_hbm, cor_hbm, np_hbm, sp_hbm, rp_hbm,
     out_ref,
     prog_v, met_v, cor_v, np_v, sp_v, rp_v,
-    f_v, ct_v, w_v, s_v, a_v, r_v, acc_v, inv_v, ids_v, out_b, in_b,
+    f_v, ct_v, co_v, w_v, s_v, a_v, r_v, acc_v, inv_v, ids_v, out_b, in_b,
     in_sem, send_sem, recv_sem,
 ):
     n_face, n_sub = sizes
@@ -126,22 +128,28 @@
         t = lax.rem(me + (offset + total), total)
         return (t // n_sub, lax.rem(t, n_sub))
 
+    barrier = pltpu.get_barrier_semaphore()
     loads = []
     for i, (src, dst) in enumerate(
         ((np_hbm, np_v), (sp_hbm, sp_v), (rp_hbm, rp_v), (met_hbm, met_v), (cor_hbm, cor_v))
     ):
         loads.append(pltpu.make_async_copy(src, dst, in_sem.at[i]))
-    for f in range(3):
-        loads.append(pltpu.make_async_copy(prog_hbm.at[f], prog_v.at[f], in_sem.at[5 + f]))
+    for k in range(BLOCKS):
+        for f in range(3):
+            rows = pl.ds(BROWS * k, BROWS)
+            loads.append(
+                pltpu.make_async_copy(
+                    prog_hbm.at[f, rows], prog_v.at[f, rows], in_sem.at[5 + 3 * k + f]
+                )
+            )
     for load in loads:
         load.start()
-
-    barrier = pltpu.get_barrier_semaphore()
     for offset in offsets:
         pl.semaphore_signal(barrier, inc=1, device_id=device(offset), device_id_type=MESH)
 
     def remote(f, g):
-        group, _, _, row, rows = g
+        group, _, count, row = g
+        rows = count + 1 if f == 0 else count
         return pltpu.make_async_remote_copy(
             src_ref=out_b.at[f, pl.ds(row, rows)],
             dst_ref=in_b.at[f, pl.ds(row, rows)],
@@ -151,17 +159,28 @@
             device_id_type=MESH,
         )
 
+    edges = sorted((row, row + count) for _, _, count, row in GROUPS)
+    for f in range(3):
+        for (_, end), nxt in zip(edges, [e[0] for e in edges[1:]] + [ROWS]):
+            end = end + 1 if f == 0 else end
+            if nxt > end:
+                in_b[f, end:nxt, :] = jnp.zeros((nxt - end, LEV), jnp.float32)
+
     for load in loads[:3]:
         load.wait()
     ids = np_v[...]
     ids2 = jnp.concatenate([ids, ids], axis=1)
     ids_v[...] = ids2
-    half = lane_iota((8, LEV)) < ELEMS
+    rolled = [ids2 if i == 0 else pltpu.roll(ids2, 16 * i, 1) for i in range(4)]
+    sub = lax.broadcasted_iota(jnp.int32, (8, LEV), 0)
+    own = sub == lane_iota((8, LEV)) // BLK
     id_rows = []
-    for j in range(8):
-        even = jnp.broadcast_to(ids2[2 * j : 2 * j + 1], (8, LEV))
-        odd = jnp.broadcast_to(ids2[2 * j + 1 : 2 * j + 2], (8, LEV))
-        id_rows.append(jnp.where(half, even, odd)[0:1])
+    for k in range(BLOCKS):
+        for h in range(2):
+            pick = rolled[(-k) % 4][8 * h : 8 * h + 8]
+            for i in range(1, 4):
+                pick = jnp.where(sub % 4 == i, rolled[(i - k) % 4][8 * h : 8 * h + 8], pick)
+            id_rows.append(jnp.sum(jnp.where(own, pick, 0), axis=0, keepdims=True))
     send_row = padded_slots(sp_v)
     recv_row = padded_slots(rp_v)
     for chunk in range(2):
@@ -185,101 +204,113 @@
     )
     ct_v[...] = jnp.transpose(coefs)
 
-    for f in range(3):
-        loads[5 + f].wait()
-        f_v[NODES * f : NODES * f + NODES] = prog_v[f].astype(jnp.float32)
-
-    def fields_of(k):
-        base = k * (BLK * 16)
-        return [
-            [f_v[pl.ds(f * NODES + base + n, BLK, stride=16), :] for n in range(16)]
-            for f in range(3)
-        ]
-
-    def spread(ct, q, n):
-        i = q * 16 + n
-        return jnp.broadcast_to(ct[:, i : i + 1], (BLK, LEV))
-
     def rows_of(k, n):
-        return pl.ds(pl.multiple_of(n * ELEMS + k * BLK, BLK), BLK)
-
-    def first_pass(k, carry):
-        u1, u2, phi = fields_of(k)
-        ct = ct_v[pl.ds(pl.multiple_of(k * BLK, BLK), BLK), :]
-        con1, con2 = [], []
-        low = lane_iota((BLK, LEV)) < 64
-        for n in range(16):
-            f1 = phi[n] * u1[n]
-            f2 = phi[n] * u2[n]
-            con1.append(spread(ct, 0, n) * f1 + spread(ct, 1, n) * f2)
-            con2.append(spread(ct, 2, n) * f1 + spread(ct, 3, n) * f2)
-            mass = spread(ct, 5, n)
-            high = mass.astype(jnp.bfloat16).astype(jnp.float32)
-            w_v[rows_of(k, n), 128:256] = jnp.where(low, high, mass - high).astype(jnp.bfloat16)
-        d1 = along_cols(con1)
-        d2 = along_rows(con2)
-        for n in range(16):
-            w_v[rows_of(k, n), 0:128] = (-NODE_W[n] * (d1[n] + d2[n])).astype(jnp.bfloat16)
-        return carry
-
-    lax.fori_loop(0, ELEMS // BLK, first_pass, 0)
-
-    sent = jnp.dot(s_v[...], w_v[:, 0:256], preferred_element_type=jnp.float32)
-    out_b[0] = sent[:, 0:128]
-    weight = sent[:, 128:256]
+        first = k * BROWS + n * BLK
+        return pl.ds(first if isinstance(first, int) else pl.multiple_of(first, BLK), BLK)
+
+    ct = ct_v[...]
+    low = lane_iota((ELEMS, LEV)) < 64
+    for n in range(16):
+        for q in range(6):
+            wide = jnp.broadcast_to(ct[:, q * 16 + n : q * 16 + n + 1], (ELEMS, LEV))
+            if q == 5:
+                high = wide.astype(jnp.bfloat16).astype(jnp.float32)
+                wide = jnp.where(low, high, wide - high).astype(jnp.bfloat16)
+            for k in range(BLOCKS):
+                part = wide[BLK * k : BLK * k + BLK]
+                if q == 5:
+                    w_v[rows_of(k, n), 128:256] = part
+                else:
+                    co_v[q, rows_of(k, n), :] = part
+
+    weight = jnp.dot(s_v[...], w_v[:, 128:256], preferred_element_type=jnp.float32)
     weight = weight + pltpu.roll(weight, 64, 1)
     diagonal = lax.broadcasted_iota(jnp.int32, (128, 128), 0) == lane_iota((128, 128))
     for chunk in range(2):
         row = jnp.sum(
             jnp.where(diagonal, weight[128 * chunk : 128 * chunk + 128], 0.0), axis=0, keepdims=True
         )
-        for _, _, count, first, _ in GROUPS:
+        for _, _, count, first in GROUPS:
             if first // 128 == chunk:
                 out_b[0, first + count : first + count + 1, :] = row
+
+    def fields_of(k):
+        return [
+            [f_v[pl.ds(f * NODES + k * BROWS + n, BLK, stride=16), :] for n in range(16)]
+            for f in range(3)
+        ]
+
+    sent = jnp.zeros((ROWS, LEV), jnp.float32)
+    for k in range(BLOCKS):
+        for f in range(3):
+            loads[5 + 3 * k + f].wait()
+            f_v[f * NODES + k * BROWS : f * NODES + k * BROWS + BROWS] = prog_v[
+                f, BROWS * k : BROWS * k + BROWS
+            ].astype(jnp.float32)
+        u1, u2, phi = fields_of(k)
+        con1, con2 = [], []
+        for n in range(16):
+            f1 = phi[n] * u1[n]
+            f2 = phi[n] * u2[n]
+            con1.append(co_v[0, rows_of(k, n), :] * f1 + co_v[1, rows_of(k, n), :] * f2)
+            con2.append(co_v[2, rows_of(k, n), :] * f1 + co_v[3, rows_of(k, n), :] * f2)
+        d1 = along_cols(con1)
+        d2 = along_rows(con2)
+        for n in range(16):
+            w_v[rows_of(k, n), 0:128] = (-NODE_W[n] * (d1[n] + d2[n])).astype(jnp.bfloat16)
+        sent = sent + jnp.dot(
+            s_v[:, BROWS * k : BROWS * k + BROWS],
+            w_v[BROWS * k : BROWS * k + BROWS, 0:128],
+            preferred_element_type=jnp.float32,
+        )
+    for _, _, count, row in GROUPS:
+        out_b[0, row : row + count, :] = sent[row : row + count]
     pl.semaphore_wait(barrier, len(offsets))
     for g in GROUPS:
         remote(0, g).start()
 
     def second_pass(k, carry):
         u1, u2, phi = fields_of(k)
-        ct = ct_v[pl.ds(pl.multiple_of(k * BLK, BLK), BLK), :]
         energy, cov1, cov2 = [], [], []
         for n in range(16):
+            rows = rows_of(k, n)
             energy.append(0.5 * (u1[n] * u1[n] + u2[n] * u2[n]) + phi[n])
-            cov1.append(spread(ct, 3, n) * u1[n] - spread(ct, 2, n) * u2[n])
-            cov2.append(spread(ct, 0, n) * u2[n] - spread(ct, 1, n) * u1[n])
+            cov1.append(co_v[3, rows, :] * u1[n] - co_v[2, rows, :] * u2[n])
+            cov2.append(co_v[0, rows, :] * u2[n] - co_v[1, rows, :] * u1[n])
         curl1 = along_cols(cov2)
         curl2 = along_rows(cov1)
         e1 = along_cols(energy)
         e2 = along_rows(energy)
         for n in range(16):
-            eta = NODE_W[n] * (curl1[n] - curl2[n]) + spread(ct, 4, n)
-            grad1 = spread(ct, 0, n) * e1[n] + spread(ct, 2, n) * e2[n]
-            grad2 = spread(ct, 1, n) * e1[n] + spread(ct, 3, n) * e2[n]
-            w_v[rows_of(k, n), 256:384] = (eta * u2[n] - NODE_W[n] * grad1).astype(jnp.bfloat16)
-            w_v[rows_of(k, n), 384:512] = (-eta * u1[n] - NODE_W[n] * grad2).astype(jnp.bfloat16)
+            rows = rows_of(k, n)
+            eta = NODE_W[n] * (curl1[n] - curl2[n]) + co_v[4, rows, :]
+            grad1 = co_v[0, rows, :] * e1[n] + co_v[2, rows, :] * e2[n]
+            grad2 = co_v[1, rows, :] * e1[n] + co_v[3, rows, :] * e2[n]
+            w_v[rows, 256:384] = (eta * u2[n] - NODE_W[n] * grad1).astype(jnp.bfloat16)
+            w_v[rows, 384:512] = (-eta * u1[n] - NODE_W[n] * grad2).astype(jnp.bfloat16)
         return carry
 
-    lax.fori_loop(0, ELEMS // BLK, second_pass, 0)
+    lax.fori_loop(0, BLOCKS, second_pass, 0)
     sent = jnp.dot(s_v[...], w_v[:, 256:512], preferred_element_type=jnp.float32)
     for f in (1, 2):
         out_b[f] = sent[:, 128 * (f - 1) : 128 * f]
         for g in GROUPS:
             remote(f, g).start()
 
-    def table(e, carry):
-        x = ids_v[...]
-        col = jnp.broadcast_to(pltpu.roll(x, LEV - e, 1)[:, 0:1], (16, LEV))
-        rows = pl.ds(pl.multiple_of(e * 16, 16), 16)
-        for j in range(8):
-            a_v[rows, 128 * j : 128 * j + 128] = one_hot(col, id_rows[j])
-        for chunk in range(2):
-            r_v[rows, 128 * chunk : 128 * chunk + 128] = one_hot(
-                col, recv_row[0:1, 128 * chunk : 128 * chunk + 128]
-            )
+    def table(i, carry):
+        x = pltpu.roll(ids_v[...], LEV - 8 * i, 1)
+        for lane in range(8):
+            col = jnp.broadcast_to(x[:, lane : lane + 1], (16, LEV))
+            rows = pl.ds(pl.multiple_of(i * 128 + lane * 16, 16), 16)
+            for j in range(8):
+                a_v[rows, 128 * j : 128 * j + 128] = one_hot(col, id_rows[j])
+            for chunk in range(2):
+                r_v[rows, 128 * chunk : 128 * chunk + 128] = one_hot(
+                    col, recv_row[0:1, 128 * chunk : 128 * chunk + 128]
+                )
         return carry
 
-    lax.fori_loop(0, ELEMS, table, 0)
+    lax.fori_loop(0, ELEMS // 8, table, 0)
 
     def gather(i, carry):
         rows = pl.ds(pl.multiple_of(i * 256, 256), 256)
@@ -289,14 +320,15 @@
     lax.fori_loop(0, NODES // 256, gather, 0)
 
     def finish(f, cols):
+        at = (f + 2) % 3
+        arrived = in_b[f].astype(jnp.bfloat16)
+
         def body(i, carry):
             rows = pl.ds(pl.multiple_of(i * 256, 256), 256)
-            got = jnp.dot(
-                r_v[rows, :], in_b[f].astype(jnp.bfloat16), preferred_element_type=jnp.float32
-            )
+            got = jnp.dot(r_v[rows, :], arrived, preferred_element_type=jnp.float32)
             got = got + acc_v[rows, cols : cols + 128]
-            field = prog_v[(f + 2) % 3, rows, :].astype(jnp.float32)
-            out_ref[(f + 2) % 3, rows, :] = (field + got * inv_v[rows, :]).astype(jnp.bfloat16)
+            field = prog_v[at, rows, :].astype(jnp.float32)
+            out_ref[at, rows, :] = (field + got * inv_v[rows, :]).astype(jnp.bfloat16)
             return carry
 
         lax.fori_loop(0, NODES // 256, body, 0)
@@ -308,7 +340,7 @@
     blocks = []
     for chunk in range(2):
         row = jnp.zeros((1, 128), jnp.float32)
-        for _, _, count, first, _ in GROUPS:
+        for _, _, count, first in GROUPS:
             if first // 128 == chunk:
                 at = first % 128
                 row = jnp.where(
@@ -344,8 +376,8 @@
     def local(prognostic, metric, coriolis, node_point, send_point, recv_point):
         result = pl.pallas_call(
             functools.partial(kernel, sizes),
-            out_shape=jax.ShapeDtypeStruct((3, NODES, LEV), jnp.bfloat16),
-            in_specs=[pl.BlockSpec(memory_space=pl.ANY)] * 6,
+            out_shape=pltpu.VMEM((3, NODES, LEV), jnp.bfloat16),
+            in_specs=[pl.BlockSpec(memory_space=pltpu.HBM)] * 6,
             out_specs=pl.BlockSpec(memory_space=pltpu.VMEM),
             scratch_shapes=[
                 pltpu.VMEM((3, NODES, LEV), jnp.bfloat16),
@@ -356,6 +388,7 @@
                 pltpu.VMEM((1, LINKS), jnp.int32),
                 pltpu.VMEM((3 * NODES, LEV), jnp.float32),
                 pltpu.VMEM((ELEMS, 128), jnp.float32),
+                pltpu.VMEM((5, NODES, LEV), jnp.float32),
                 pltpu.VMEM((NODES, 512), jnp.bfloat16),
                 pltpu.VMEM((ROWS, NODES), jnp.bfloat16),
                 pltpu.VMEM((NODES, NODES), jnp.bfloat16),
@@ -365,18 +398,20 @@
                 pltpu.VMEM((16, LEV), jnp.int32),
                 pltpu.VMEM((3, ROWS, LEV), jnp.float32),
                 pltpu.VMEM((3, ROWS, LEV), jnp.float32),
-                pltpu.SemaphoreType.DMA((8,)),
+                pltpu.SemaphoreType.DMA((5 + 3 * BLOCKS,)),
                 pltpu.SemaphoreType.DMA((3, 8)),
                 pltpu.SemaphoreType.DMA((3, 8)),
             ],
-            compiler_params=pltpu.CompilerParams(collective_id=0, has_side_effects=True),
+            compiler_params=pltpu.CompilerParams(
+                collective_id=0, has_side_effects=True, vmem_limit_bytes=40 * 1024 * 1024
+            ),
         )(
-            prognostic.reshape(3, NODES, LEV),
-            jnp.transpose(metric, (0, 2, 1)),
-            jnp.transpose(coriolis),
-            jnp.transpose(node_point),
-            send_point.reshape(1, LINKS),
-            recv_point.reshape(1, LINKS),
+            pltpu.with_memory_space_constraint(prognostic.reshape(3, NODES, LEV), pltpu.HBM),
+            pltpu.with_memory_space_constraint(jnp.transpose(metric, (0, 2, 1)), pltpu.HBM),
+            pltpu.with_memory_space_constraint(jnp.transpose(coriolis), pltpu.HBM),
+            pltpu.with_memory_space_constraint(jnp.transpose(node_point), pltpu.HBM),
+            pltpu.with_memory_space_constraint(send_point.reshape(1, LINKS), pltpu.HBM),
+            pltpu.with_memory_space_constraint(recv_point.reshape(1, LINKS), pltpu.HBM),
         )
         return result.reshape(3, ELEMS, 16, LEV)
 

time: 43.5 us -> 36.6 us (0.84)
  Pallas kernels: 41.1 us -> 35.6 us
  local copies, waits for them, and re-layouts: 2.15 us -> 0.88 us
    pallas_call x1, Pallas kernels: 41.1 us -> 35.6 us  [local(): pl.pallas_call(functools.partial(kernel, sizes), out_shape=pltpu.VMEM((3,...]
    unnamed x1, local copies, waits for them, and re-layouts: 2.15 us -> 0.88 us
where the time goes in v2:
time: 36.6 us; the launch traced here: 36.4 us
  Pallas kernels  35.6 us (97%)
  local copies, waits for them, and re-layouts  0.88 us (2%)
    pallas_call x1, Pallas kernels, local(): pl.pallas_call(functools.partial(kernel, sizes), out_shape=pltpu.VMEM((3,...  35.6 us
    unnamed x1, local copies, waits for them, and re-layouts  0.88 us

profile of v2, /device:TPU:1, one launch (start us, length us, event | category | flops | bytes accessed | tf_op | source)
XLA Modules:
  0.0 36.4 jit_solution(18127442137683244192)
XLA Ops:
  0.0 35.6 %shard_map.64 = bf16[3,1024,128]{2,1,0:T(8,128)(2,1)S(1)} custom-call(bf16[3,1024,128]{2,1,0:T(8,128)(2,1)} %bitcast.8, f32[4,16,64]{2,1,0:T(8,128)} %bitcast.9, f32[16,64]{1,0:T(8,128)} %bitcast.10, s32[16,64]{1,0:T(8,128)} %bitcast.11, s32[1,212]{1,0:T(1,128)} %bitcast.12, s32[1,212]{1,0:T(1,128)} %bitcast.13), custom_call_target="tpu_custom_call" | custom-call | tf_op jit(solution)/shard_map/pallas_call | solution.py:377
  35.6 0.9 %copy.8 = bf16[3,64,16,128]{3,2,1,0:T(8,128)(2,1)} copy(bf16[3,64,16,128]{3,2,1,0:T(8,128)(2,1)S(1)} %bitcast.7) | data formatting | bytes 1572864

commit v3 on v2

--- a/solution.py
+++ b/solution.py
@@ -115,7 +115,7 @@
     prog_hbm, met_hbm, cor_hbm, np_hbm, sp_hbm, rp_hbm,
     out_ref,
     prog_v, met_v, cor_v, np_v, sp_v, rp_v,
-    f_v, ct_v, co_v, w_v, s_v, a_v, r_v, acc_v, inv_v, ids_v, out_b, in_b,
+    f_v, turn_v, ct_v, co_v, w_v, s_v, a_v, r_v, acc_v, inv_v, ids_v, out_b, in_b, out_w, in_w,
     in_sem, send_sem, recv_sem,
 ):
     n_face, n_sub = sizes
@@ -129,42 +129,48 @@
         return (t // n_sub, lax.rem(t, n_sub))
 
     barrier = pltpu.get_barrier_semaphore()
+    for offset in offsets:
+        pl.semaphore_signal(barrier, inc=1, device_id=device(offset), device_id_type=MESH)
     loads = []
     for i, (src, dst) in enumerate(
         ((np_hbm, np_v), (sp_hbm, sp_v), (rp_hbm, rp_v), (met_hbm, met_v), (cor_hbm, cor_v))
     ):
         loads.append(pltpu.make_async_copy(src, dst, in_sem.at[i]))
-    for k in range(BLOCKS):
-        for f in range(3):
-            rows = pl.ds(BROWS * k, BROWS)
-            loads.append(
-                pltpu.make_async_copy(
-                    prog_hbm.at[f, rows], prog_v.at[f, rows], in_sem.at[5 + 3 * k + f]
-                )
+    for f in range(3):
+        loads.append(
+            pltpu.make_async_copy(
+                prog_hbm.at[f], prog_v.at[:, pl.ds(LEV * f, LEV)], in_sem.at[5 + f]
             )
+        )
     for load in loads:
         load.start()
-    for offset in offsets:
-        pl.semaphore_signal(barrier, inc=1, device_id=device(offset), device_id_type=MESH)
 
     def remote(f, g):
         group, _, count, row = g
-        rows = count + 1 if f == 0 else count
         return pltpu.make_async_remote_copy(
-            src_ref=out_b.at[f, pl.ds(row, rows)],
-            dst_ref=in_b.at[f, pl.ds(row, rows)],
+            src_ref=out_b.at[f, pl.ds(row, count)],
+            dst_ref=in_b.at[f, pl.ds(row, count)],
             send_sem=send_sem.at[f, group],
             recv_sem=recv_sem.at[f, group],
             device_id=device(offsets[group]),
             device_id_type=MESH,
         )
 
+    def remote_weights(g):
+        group, _, _, row = g
+        return pltpu.make_async_remote_copy(
+            src_ref=out_w.at[row // 128],
+            dst_ref=in_w.at[group],
+            send_sem=send_sem.at[3, group],
+            recv_sem=recv_sem.at[3, group],
+            device_id=device(offsets[group]),
+            device_id_type=MESH,
+        )
+
     edges = sorted((row, row + count) for _, _, count, row in GROUPS)
     for f in range(3):
         for (_, end), nxt in zip(edges, [e[0] for e in edges[1:]] + [ROWS]):
-            end = end + 1 if f == 0 else end
-            if nxt > end:
-                in_b[f, end:nxt, :] = jnp.zeros((nxt - end, LEV), jnp.float32)
+            in_b[f, end:nxt, :] = jnp.zeros((nxt - end, LEV), jnp.float32)
 
     for load in loads[:3]:
         load.wait()
@@ -223,30 +229,21 @@
                 else:
                     co_v[q, rows_of(k, n), :] = part
 
-    weight = jnp.dot(s_v[...], w_v[:, 128:256], preferred_element_type=jnp.float32)
-    weight = weight + pltpu.roll(weight, 64, 1)
-    diagonal = lax.broadcasted_iota(jnp.int32, (128, 128), 0) == lane_iota((128, 128))
-    for chunk in range(2):
-        row = jnp.sum(
-            jnp.where(diagonal, weight[128 * chunk : 128 * chunk + 128], 0.0), axis=0, keepdims=True
-        )
-        for _, _, count, first in GROUPS:
-            if first // 128 == chunk:
-                out_b[0, first + count : first + count + 1, :] = row
+    at = lax.broadcasted_iota(jnp.int32, (BROWS, BROWS), 0)
+    turn_v[...] = one_hot(at % BLK * 16 + at // BLK, lane_iota((BROWS, BROWS)))
+
+    for load in loads[5:]:
+        load.wait()
+    for k in range(BLOCKS):
+        rows = slice(BROWS * k, BROWS * k + BROWS)
+        f_v[rows, :] = jnp.dot(turn_v[...], prog_v[rows, :], preferred_element_type=jnp.float32)
 
     def fields_of(k):
         return [
-            [f_v[pl.ds(f * NODES + k * BROWS + n, BLK, stride=16), :] for n in range(16)]
-            for f in range(3)
+            [f_v[rows_of(k, n), LEV * f : LEV * f + LEV] for n in range(16)] for f in range(3)
         ]
 
-    sent = jnp.zeros((ROWS, LEV), jnp.float32)
     for k in range(BLOCKS):
-        for f in range(3):
-            loads[5 + 3 * k + f].wait()
-            f_v[f * NODES + k * BROWS : f * NODES + k * BROWS + BROWS] = prog_v[
-                f, BROWS * k : BROWS * k + BROWS
-            ].astype(jnp.float32)
         u1, u2, phi = fields_of(k)
         con1, con2 = [], []
         for n in range(16):
@@ -258,16 +255,21 @@
         d2 = along_rows(con2)
         for n in range(16):
             w_v[rows_of(k, n), 0:128] = (-NODE_W[n] * (d1[n] + d2[n])).astype(jnp.bfloat16)
-        sent = sent + jnp.dot(
-            s_v[:, BROWS * k : BROWS * k + BROWS],
-            w_v[BROWS * k : BROWS * k + BROWS, 0:128],
-            preferred_element_type=jnp.float32,
-        )
-    for _, _, count, row in GROUPS:
-        out_b[0, row : row + count, :] = sent[row : row + count]
+    sent = jnp.dot(s_v[...], w_v[:, 0:256], preferred_element_type=jnp.float32)
+    out_b[0] = sent[:, 0:128]
     pl.semaphore_wait(barrier, len(offsets))
     for g in GROUPS:
         remote(0, g).start()
+
+    weight = sent[:, 128:256]
+    weight = weight + pltpu.roll(weight, 64, 1)
+    diagonal = lax.broadcasted_iota(jnp.int32, (128, 128), 0) == lane_iota((128, 128))
+    for chunk in range(2):
+        out_w[chunk] = jnp.sum(
+            jnp.where(diagonal, weight[128 * chunk : 128 * chunk + 128], 0.0), axis=0, keepdims=True
+        )
+    for g in GROUPS:
+        remote_weights(g).start()
 
     def second_pass(k, carry):
         u1, u2, phi = fields_of(k)
@@ -294,8 +296,16 @@
     sent = jnp.dot(s_v[...], w_v[:, 256:512], preferred_element_type=jnp.float32)
     for f in (1, 2):
         out_b[f] = sent[:, 128 * (f - 1) : 128 * f]
-        for g in GROUPS:
-            remote(f, g).start()
+
+    face = lax.axis_index("face")
+    turn = lax.rem(face // 2, 2) * 2 + 1 - lax.rem(face, 2)
+
+    def send_wind():
+        for f in (1, 2):
+            for g in GROUPS:
+                remote(f, g).start()
+
+    pl.when(turn == 0)(send_wind)
 
     def table(i, carry):
         x = pltpu.roll(ids_v[...], LEV - 8 * i, 1)
@@ -311,6 +321,7 @@
         return carry
 
     lax.fori_loop(0, ELEMS // 8, table, 0)
+    pl.when((turn == 1) | (turn == 2))(send_wind)
 
     def gather(i, carry):
         rows = pl.ds(pl.multiple_of(i * 256, 256), 256)
@@ -318,56 +329,43 @@
         return carry
 
     lax.fori_loop(0, NODES // 256, gather, 0)
+    pl.when(turn == 3)(send_wind)
 
     def finish(f, cols):
         at = (f + 2) % 3
-        arrived = in_b[f].astype(jnp.bfloat16)
-
-        def body(i, carry):
-            rows = pl.ds(pl.multiple_of(i * 256, 256), 256)
-            got = jnp.dot(r_v[rows, :], arrived, preferred_element_type=jnp.float32)
-            got = got + acc_v[rows, cols : cols + 128]
-            field = prog_v[at, rows, :].astype(jnp.float32)
-            out_ref[at, rows, :] = (field + got * inv_v[rows, :]).astype(jnp.bfloat16)
-            return carry
-
-        lax.fori_loop(0, NODES // 256, body, 0)
+        got = jnp.dot(
+            r_v[...], in_b[f].astype(jnp.bfloat16), preferred_element_type=jnp.float32
+        )
+        got = (got + acc_v[:, cols : cols + 128]) * inv_v[...]
+        field = prog_v[:, LEV * at : LEV * at + LEV].astype(jnp.float32)
+        out_ref[at] = (field + got).astype(jnp.bfloat16)
 
     for g in GROUPS:
-        remote(0, g).wait_recv()
+        remote_weights(g).wait_recv()
     lane = lane_iota((1, 128))
     low = lane_iota((128, 128)) < 64
     blocks = []
     for chunk in range(2):
         row = jnp.zeros((1, 128), jnp.float32)
-        for _, _, count, first in GROUPS:
+        for group, _, count, first in GROUPS:
             if first // 128 == chunk:
                 at = first % 128
-                row = jnp.where(
-                    (lane >= at) & (lane < at + count), in_b[0, first + count : first + count + 1, :], row
-                )
+                row = jnp.where((lane >= at) & (lane < at + count), in_w[group], row)
         col = jnp.transpose(jnp.broadcast_to(row, (128, 128)))
         high = col.astype(jnp.bfloat16).astype(jnp.float32)
         blocks.append(jnp.where(low, high, col - high).astype(jnp.bfloat16))
     arrived = jnp.concatenate(blocks, axis=0)
 
-    def weights(i, carry):
-        rows = pl.ds(pl.multiple_of(i * 256, 256), 256)
-        w = jnp.dot(r_v[rows, :], arrived, preferred_element_type=jnp.float32)
-        w = w + acc_v[rows, 128:256]
-        w = w + pltpu.roll(w, 64, 1)
-        inv_v[rows, :] = STEP_SIZE / w
-        return carry
-
-    lax.fori_loop(0, NODES // 256, weights, 0)
-    finish(0, 0)
-    for f in (1, 2):
+    weight = jnp.dot(r_v[...], arrived, preferred_element_type=jnp.float32) + acc_v[:, 128:256]
+    inv_v[...] = STEP_SIZE / (weight + pltpu.roll(weight, 64, 1))
+    for f in range(3):
         for g in GROUPS:
             remote(f, g).wait_recv()
-        finish(f, 128 + 128 * f)
-    for f in range(3):
-        for g in GROUPS:
+        finish(f, 128 * f + 128 if f else 0)
+    for g in GROUPS:
+        for f in range(3):
             remote(f, g).wait_send()
+        remote_weights(g).wait_send()
 
 
 def solution(mesh):
@@ -380,13 +378,14 @@
             in_specs=[pl.BlockSpec(memory_space=pltpu.HBM)] * 6,
             out_specs=pl.BlockSpec(memory_space=pltpu.VMEM),
             scratch_shapes=[
-                pltpu.VMEM((3, NODES, LEV), jnp.bfloat16),
+                pltpu.VMEM((NODES, 3 * LEV), jnp.bfloat16),
                 pltpu.VMEM((4, 16, ELEMS), jnp.float32),
                 pltpu.VMEM((16, ELEMS), jnp.float32),
                 pltpu.VMEM((16, ELEMS), jnp.int32),
                 pltpu.VMEM((1, LINKS), jnp.int32),
                 pltpu.VMEM((1, LINKS), jnp.int32),
-                pltpu.VMEM((3 * NODES, LEV), jnp.float32),
+                pltpu.VMEM((NODES, 3 * LEV), jnp.float32),
+                pltpu.VMEM((BROWS, BROWS), jnp.bfloat16),
                 pltpu.VMEM((ELEMS, 128), jnp.float32),
                 pltpu.VMEM((5, NODES, LEV), jnp.float32),
                 pltpu.VMEM((NODES, 512), jnp.bfloat16),
@@ -398,9 +397,11 @@
                 pltpu.VMEM((16, LEV), jnp.int32),
                 pltpu.VMEM((3, ROWS, LEV), jnp.float32),
                 pltpu.VMEM((3, ROWS, LEV), jnp.float32),
-                pltpu.SemaphoreType.DMA((5 + 3 * BLOCKS,)),
-                pltpu.SemaphoreType.DMA((3, 8)),
-                pltpu.SemaphoreType.DMA((3, 8)),
+                pltpu.VMEM((2, 1, LEV), jnp.float32),
+                pltpu.VMEM((8, 1, LEV), jnp.float32),
+                pltpu.SemaphoreType.DMA((8,)),
+                pltpu.SemaphoreType.DMA((4, 8)),
+                pltpu.SemaphoreType.DMA((4, 8)),
             ],
             compiler_params=pltpu.CompilerParams(
                 collective_id=0, has_side_effects=True, vmem_limit_bytes=40 * 1024 * 1024

time: 36.6 us -> 34.5 us (0.943)
  Pallas kernels: 35.6 us -> 33.5 us
    pallas_call x1, Pallas kernels: 35.6 us -> 33.5 us  [local(): pl.pallas_call(functools.partial(kernel, sizes), out_shape=pltpu.VMEM((3,...]
where the time goes in v3:
time: 34.5 us; the launch traced here: 34.4 us
  Pallas kernels  33.5 us (97%)
  local copies, waits for them, and re-layouts  0.88 us (3%)
    pallas_call x1, Pallas kernels, local(): pl.pallas_call(functools.partial(kernel, sizes), out_shape=pltpu.VMEM((3,...  33.5 us
    unnamed x1, local copies, waits for them, and re-layouts  0.88 us

profile of v3, /device:TPU:1, one launch (start us, length us, event | category | flops | bytes accessed | tf_op | source)
XLA Modules:
  0.0 34.4 jit_solution(6510918358095198461)
XLA Ops:
  0.0 33.5 %shard_map.64 = bf16[3,1024,128]{2,1,0:T(8,128)(2,1)S(1)} custom-call(bf16[3,1024,128]{2,1,0:T(8,128)(2,1)} %bitcast.8, f32[4,16,64]{2,1,0:T(8,128)} %bitcast.9, f32[16,64]{1,0:T(8,128)} %bitcast.10, s32[16,64]{1,0:T(8,128)} %bitcast.11, s32[1,212]{1,0:T(1,128)} %bitcast.12, s32[1,212]{1,0:T(1,128)} %bitcast.13), custom_call_target="tpu_custom_call" | custom-call | tf_op jit(solution)/shard_map/pallas_call | solution.py:375
  33.5 0.9 %copy.8 = bf16[3,64,16,128]{3,2,1,0:T(8,128)(2,1)} copy(bf16[3,64,16,128]{3,2,1,0:T(8,128)(2,1)S(1)} %bitcast.7) | data formatting | bytes 1572864

commit v4 on v3

--- a/solution.py
+++ b/solution.py
@@ -21,6 +21,7 @@
 STEP_SIZE = 0.1
 BLK = 16
 BLOCKS = ELEMS // BLK
+PLANES = 16
 BROWS = 16 * BLK
 
 GROUPS = (
@@ -257,19 +258,10 @@
             w_v[rows_of(k, n), 0:128] = (-NODE_W[n] * (d1[n] + d2[n])).astype(jnp.bfloat16)
     sent = jnp.dot(s_v[...], w_v[:, 0:256], preferred_element_type=jnp.float32)
     out_b[0] = sent[:, 0:128]
-    pl.semaphore_wait(barrier, len(offsets))
-    for g in GROUPS:
-        remote(0, g).start()
-
-    weight = sent[:, 128:256]
-    weight = weight + pltpu.roll(weight, 64, 1)
-    diagonal = lax.broadcasted_iota(jnp.int32, (128, 128), 0) == lane_iota((128, 128))
-    for chunk in range(2):
-        out_w[chunk] = jnp.sum(
-            jnp.where(diagonal, weight[128 * chunk : 128 * chunk + 128], 0.0), axis=0, keepdims=True
-        )
-    for g in GROUPS:
-        remote_weights(g).start()
+    def send(fields, groups):
+        for f in fields:
+            for g in groups:
+                remote(f, g).start()
 
     def second_pass(k, carry):
         u1, u2, phi = fields_of(k)
@@ -292,20 +284,11 @@
             w_v[rows, 384:512] = (-eta * u1[n] - NODE_W[n] * grad2).astype(jnp.bfloat16)
         return carry
 
-    lax.fori_loop(0, BLOCKS, second_pass, 0)
-    sent = jnp.dot(s_v[...], w_v[:, 256:512], preferred_element_type=jnp.float32)
-    for f in (1, 2):
-        out_b[f] = sent[:, 128 * (f - 1) : 128 * f]
-
-    face = lax.axis_index("face")
-    turn = lax.rem(face // 2, 2) * 2 + 1 - lax.rem(face, 2)
-
-    def send_wind():
+    def wind():
+        lax.fori_loop(0, BLOCKS, second_pass, 0)
+        sent = jnp.dot(s_v[...], w_v[:, 256:512], preferred_element_type=jnp.float32)
         for f in (1, 2):
-            for g in GROUPS:
-                remote(f, g).start()
-
-    pl.when(turn == 0)(send_wind)
+            out_b[f] = sent[:, 128 * (f - 1) : 128 * f]
 
     def table(i, carry):
         x = pltpu.roll(ids_v[...], LEV - 8 * i, 1)
@@ -320,16 +303,53 @@
                 )
         return carry
 
-    lax.fori_loop(0, ELEMS // 8, table, 0)
-    pl.when((turn == 1) | (turn == 2))(send_wind)
+    def tables():
+        lax.fori_loop(0, ELEMS // 8, table, 0)
 
     def gather(i, carry):
         rows = pl.ds(pl.multiple_of(i * 256, 256), 256)
         acc_v[rows, :] = jnp.dot(a_v[rows, :], w_v[...], preferred_element_type=jnp.float32)
         return carry
 
-    lax.fori_loop(0, NODES // 256, gather, 0)
-    pl.when(turn == 3)(send_wind)
+    def sums():
+        lax.fori_loop(0, NODES // 256, gather, 0)
+
+    face = lax.axis_index("face")
+    plane = lax.rem(face // 2, PLANES)
+    first = plane < 4
+
+    @pl.when(first)
+    def _():
+        wind()
+        tables()
+        sums()
+
+    pl.semaphore_wait(barrier, len(offsets))
+    send((0,), GROUPS)
+    weight = sent[:, 128:256]
+    weight = weight + pltpu.roll(weight, 64, 1)
+    diagonal = lax.broadcasted_iota(jnp.int32, (128, 128), 0) == lane_iota((128, 128))
+    for chunk in range(2):
+        out_w[chunk] = jnp.sum(
+            jnp.where(diagonal, weight[128 * chunk : 128 * chunk + 128], 0.0), axis=0, keepdims=True
+        )
+    for g in GROUPS:
+        remote_weights(g).start()
+
+    @pl.when(first)
+    def _():
+        send((1, 2), GROUPS)
+
+    @pl.when(jnp.logical_not(first))
+    def _():
+        turn = lax.rem(plane, 2) * 2 + 1 - lax.rem(face, 2)
+        wind()
+        pl.when(turn == 0)(lambda: send((1, 2), GROUPS[:2]))
+        send((1, 2), GROUPS[2:])
+        tables()
+        pl.when((turn == 1) | (turn == 2))(lambda: send((1, 2), GROUPS[:2]))
+        sums()
+        pl.when(turn == 3)(lambda: send((1, 2), GROUPS[:2]))
 
     def finish(f, cols):
         at = (f + 2) % 3

time: 34.5 us -> 32.6 us (0.945)
  Pallas kernels: 33.5 us -> 31.5 us
    pallas_call x1, Pallas kernels: 33.5 us -> 31.5 us  [local(): pl.pallas_call(functools.partial(kernel, sizes), out_shape=pltpu.VMEM((3,...]
where the time goes in v4:
time: 32.6 us; the launch traced here: 32.4 us
  Pallas kernels  31.5 us (97%)
  local copies, waits for them, and re-layouts  0.88 us (3%)
    pallas_call x1, Pallas kernels, local(): pl.pallas_call(functools.partial(kernel, sizes), out_shape=pltpu.VMEM((3,...  31.5 us
    unnamed x1, local copies, waits for them, and re-layouts  0.88 us

profile of v4, /device:TPU:1, one launch (start us, length us, event | category | flops | bytes accessed | tf_op | source)
XLA Modules:
  0.0 32.4 jit_solution(9433266691605349027)
XLA Ops:
  0.0 31.5 %shard_map.64 = bf16[3,1024,128]{2,1,0:T(8,128)(2,1)S(1)} custom-call(bf16[3,1024,128]{2,1,0:T(8,128)(2,1)} %bitcast.8, f32[4,16,64]{2,1,0:T(8,128)} %bitcast.9, f32[16,64]{1,0:T(8,128)} %bitcast.10, s32[16,64]{1,0:T(8,128)} %bitcast.11, s32[1,212]{1,0:T(1,128)} %bitcast.12, s32[1,212]{1,0:T(1,128)} %bitcast.13), custom_call_target="tpu_custom_call" | custom-call | tf_op jit(solution)/shard_map/pallas_call | solution.py:395
  31.6 0.9 %copy.8 = bf16[3,64,16,128]{3,2,1,0:T(8,128)(2,1)} copy(bf16[3,64,16,128]{3,2,1,0:T(8,128)(2,1)S(1)} %bitcast.7) | data formatting | bytes 1572864

commit v5 on v4

--- a/solution.py
+++ b/solution.py
@@ -21,6 +21,8 @@
 STEP_SIZE = 0.1
 BLK = 16
 BLOCKS = ELEMS // BLK
+HALF = NODES // 2
+MASS = 5
 PLANES = 16
 BROWS = 16 * BLK
 
@@ -137,12 +139,14 @@
         ((np_hbm, np_v), (sp_hbm, sp_v), (rp_hbm, rp_v), (met_hbm, met_v), (cor_hbm, cor_v))
     ):
         loads.append(pltpu.make_async_copy(src, dst, in_sem.at[i]))
-    for f in range(3):
-        loads.append(
-            pltpu.make_async_copy(
-                prog_hbm.at[f], prog_v.at[:, pl.ds(LEV * f, LEV)], in_sem.at[5 + f]
+    for h in range(2):
+        rows = pl.ds(HALF * h, HALF)
+        for f in range(3):
+            loads.append(
+                pltpu.make_async_copy(
+                    prog_hbm.at[f, rows], prog_v.at[f, rows], in_sem.at[5 + 3 * h + f]
+                )
             )
-        )
     for load in loads:
         load.start()
 
@@ -215,29 +219,38 @@
         first = k * BROWS + n * BLK
         return pl.ds(first if isinstance(first, int) else pl.multiple_of(first, BLK), BLK)
 
-    ct = ct_v[...]
-    low = lane_iota((ELEMS, LEV)) < 64
-    for n in range(16):
-        for q in range(6):
-            wide = jnp.broadcast_to(ct[:, q * 16 + n : q * 16 + n + 1], (ELEMS, LEV))
-            if q == 5:
+    at = lax.broadcasted_iota(jnp.int32, (BROWS, BROWS), 0)
+    turn_v[...] = one_hot(at % BLK * 16 + at // BLK, lane_iota((BROWS, BROWS)))
+
+    def spread(q):
+        for n in range(16):
+            wide = jnp.broadcast_to(ct_v[:, q * 16 + n : q * 16 + n + 1], (ELEMS, LEV))
+            if q == MASS:
                 high = wide.astype(jnp.bfloat16).astype(jnp.float32)
-                wide = jnp.where(low, high, wide - high).astype(jnp.bfloat16)
+                low = lane_iota((ELEMS, LEV)) >= 64
+                wide = jnp.where(low, wide - high, high).astype(jnp.bfloat16)
             for k in range(BLOCKS):
                 part = wide[BLK * k : BLK * k + BLK]
-                if q == 5:
+                if q == MASS:
                     w_v[rows_of(k, n), 128:256] = part
                 else:
                     co_v[q, rows_of(k, n), :] = part
 
-    at = lax.broadcasted_iota(jnp.int32, (BROWS, BROWS), 0)
-    turn_v[...] = one_hot(at % BLK * 16 + at // BLK, lane_iota((BROWS, BROWS)))
-
-    for load in loads[5:]:
-        load.wait()
-    for k in range(BLOCKS):
-        rows = slice(BROWS * k, BROWS * k + BROWS)
-        f_v[rows, :] = jnp.dot(turn_v[...], prog_v[rows, :], preferred_element_type=jnp.float32)
+    def turn_half(h):
+        for load in loads[5 + 3 * h : 8 + 3 * h]:
+            load.wait()
+        for k in (2 * h, 2 * h + 1):
+            rows = slice(BROWS * k, BROWS * k + BROWS)
+            block = jnp.concatenate([prog_v[f, rows] for f in range(3)], axis=1)
+            f_v[rows, :] = jnp.dot(turn_v[...], block, preferred_element_type=jnp.float32)
+
+    spread(0)
+    spread(1)
+    turn_half(0)
+    spread(2)
+    spread(3)
+    spread(MASS)
+    turn_half(1)
 
     def fields_of(k):
         return [
@@ -258,6 +271,8 @@
             w_v[rows_of(k, n), 0:128] = (-NODE_W[n] * (d1[n] + d2[n])).astype(jnp.bfloat16)
     sent = jnp.dot(s_v[...], w_v[:, 0:256], preferred_element_type=jnp.float32)
     out_b[0] = sent[:, 0:128]
+    spread(4)
+
     def send(fields, groups):
         for f in fields:
             for g in groups:
@@ -351,14 +366,13 @@
         sums()
         pl.when(turn == 3)(lambda: send((1, 2), GROUPS[:2]))
 
-    def finish(f, cols):
-        at = (f + 2) % 3
+    columns = (slice(0, 128), slice(256, 384), slice(384, 512))
+
+    def finish(f):
         got = jnp.dot(
             r_v[...], in_b[f].astype(jnp.bfloat16), preferred_element_type=jnp.float32
         )
-        got = (got + acc_v[:, cols : cols + 128]) * inv_v[...]
-        field = prog_v[:, LEV * at : LEV * at + LEV].astype(jnp.float32)
-        out_ref[at] = (field + got).astype(jnp.bfloat16)
+        out_ref[(f + 2) % 3] = (acc_v[:, columns[f]] + got * inv_v[...]).astype(jnp.bfloat16)
 
     for g in GROUPS:
         remote_weights(g).wait_recv()
@@ -379,9 +393,12 @@
     weight = jnp.dot(r_v[...], arrived, preferred_element_type=jnp.float32) + acc_v[:, 128:256]
     inv_v[...] = STEP_SIZE / (weight + pltpu.roll(weight, 64, 1))
     for f in range(3):
+        field = prog_v[(f + 2) % 3].astype(jnp.float32)
+        acc_v[:, columns[f]] = field + acc_v[:, columns[f]] * inv_v[...]
+    for f in range(3):
         for g in GROUPS:
             remote(f, g).wait_recv()
-        finish(f, 128 * f + 128 if f else 0)
+        finish(f)
     for g in GROUPS:
         for f in range(3):
             remote(f, g).wait_send()
@@ -398,7 +415,7 @@
             in_specs=[pl.BlockSpec(memory_space=pltpu.HBM)] * 6,
             out_specs=pl.BlockSpec(memory_space=pltpu.VMEM),
             scratch_shapes=[
-                pltpu.VMEM((NODES, 3 * LEV), jnp.bfloat16),
+                pltpu.VMEM((3, NODES, LEV), jnp.bfloat16),
                 pltpu.VMEM((4, 16, ELEMS), jnp.float32),
                 pltpu.VMEM((16, ELEMS), jnp.float32),
                 pltpu.VMEM((16, ELEMS), jnp.int32),
@@ -419,7 +436,7 @@
                 pltpu.VMEM((3, ROWS, LEV), jnp.float32),
                 pltpu.VMEM((2, 1, LEV), jnp.float32),
                 pltpu.VMEM((8, 1, LEV), jnp.float32),
-                pltpu.SemaphoreType.DMA((8,)),
+                pltpu.SemaphoreType.DMA((11,)),
                 pltpu.SemaphoreType.DMA((4, 8)),
                 pltpu.SemaphoreType.DMA((4, 8)),
             ],

time: 32.6 us -> 32.5 us (level)
  no operation moved by 1% of the time
where the time goes in v5:
time: 32.5 us; the launch traced here: 32.3 us
  Pallas kernels  31.4 us (97%)
  local copies, waits for them, and re-layouts  0.88 us (3%)
    pallas_call x1, Pallas kernels, local(): pl.pallas_call(functools.partial(kernel, sizes), out_shape=pltpu.VMEM((3,...  31.4 us
    unnamed x1, local copies, waits for them, and re-layouts  0.88 us

profile of v5, /device:TPU:1, one launch (start us, length us, event | category | flops | bytes accessed | tf_op | source)
XLA Modules:
  0.0 32.3 jit_solution(5298355994340178934)
XLA Ops:
  0.0 31.4 %shard_map.64 = bf16[3,1024,128]{2,1,0:T(8,128)(2,1)S(1)} custom-call(bf16[3,1024,128]{2,1,0:T(8,128)(2,1)} %bitcast.8, f32[4,16,64]{2,1,0:T(8,128)} %bitcast.9, f32[16,64]{1,0:T(8,128)} %bitcast.10, s32[16,64]{1,0:T(8,128)} %bitcast.11, s32[1,212]{1,0:T(1,128)} %bitcast.12, s32[1,212]{1,0:T(1,128)} %bitcast.13), custom_call_target="tpu_custom_call" | custom-call | tf_op jit(solution)/shard_map/pallas_call | solution.py:412
  31.4 0.9 %copy.8 = bf16[3,64,16,128]{3,2,1,0:T(8,128)(2,1)} copy(bf16[3,64,16,128]{3,2,1,0:T(8,128)(2,1)S(1)} %bitcast.7) | data formatting | bytes 1572864

commit v6 on v5

--- a/solution.py
+++ b/solution.py
@@ -132,7 +132,8 @@
         return (t // n_sub, lax.rem(t, n_sub))
 
     barrier = pltpu.get_barrier_semaphore()
-    for offset in offsets:
+    for group in (2, 4, 6, 3, 5, 7, 0, 1):
+        offset = offsets[group]
         pl.semaphore_signal(barrier, inc=1, device_id=device(offset), device_id_type=MESH)
     loads = []
     for i, (src, dst) in enumerate(
@@ -340,7 +341,7 @@
         sums()
 
     pl.semaphore_wait(barrier, len(offsets))
-    send((0,), GROUPS)
+    send((0,), GROUPS[:2])
     weight = sent[:, 128:256]
     weight = weight + pltpu.roll(weight, 64, 1)
     diagonal = lax.broadcasted_iota(jnp.int32, (128, 128), 0) == lane_iota((128, 128))
@@ -348,11 +349,16 @@
         out_w[chunk] = jnp.sum(
             jnp.where(diagonal, weight[128 * chunk : 128 * chunk + 128], 0.0), axis=0, keepdims=True
         )
-    for g in GROUPS:
-        remote_weights(g).start()
+    def send_weights(groups):
+        for g in groups:
+            remote_weights(g).start()
+
+    send_weights(GROUPS[:2])
 
     @pl.when(first)
     def _():
+        send((0,), GROUPS[2:])
+        send_weights(GROUPS[2:])
         send((1, 2), GROUPS)
 
     @pl.when(jnp.logical_not(first))
@@ -360,7 +366,8 @@
         turn = lax.rem(plane, 2) * 2 + 1 - lax.rem(face, 2)
         wind()
         pl.when(turn == 0)(lambda: send((1, 2), GROUPS[:2]))
-        send((1, 2), GROUPS[2:])
+        send_weights(GROUPS[2:])
+        send((0, 1, 2), GROUPS[2:])
         tables()
         pl.when((turn == 1) | (turn == 2))(lambda: send((1, 2), GROUPS[:2]))
         sums()

time: 32.5 us -> 32.5 us (level)
  no operation moved by 1% of the time
where the time goes in v6:
time: 32.5 us; the launch traced here: 32.3 us
  Pallas kernels  31.4 us (97%)
  local copies, waits for them, and re-layouts  0.88 us (3%)
    pallas_call x1, Pallas kernels, local(): pl.pallas_call(functools.partial(kernel, sizes), out_shape=pltpu.VMEM((3,...  31.4 us
    unnamed x1, local copies, waits for them, and re-layouts  0.88 us

profile of v6, /device:TPU:1, one launch (start us, length us, event | category | flops | bytes accessed | tf_op | source)
XLA Modules:
  0.0 32.3 jit_solution(6527357120668823733)
XLA Ops:
  0.0 31.4 %shard_map.64 = bf16[3,1024,128]{2,1,0:T(8,128)(2,1)S(1)} custom-call(bf16[3,1024,128]{2,1,0:T(8,128)(2,1)} %bitcast.8, f32[4,16,64]{2,1,0:T(8,128)} %bitcast.9, f32[16,64]{1,0:T(8,128)} %bitcast.10, s32[16,64]{1,0:T(8,128)} %bitcast.11, s32[1,212]{1,0:T(1,128)} %bitcast.12, s32[1,212]{1,0:T(1,128)} %bitcast.13), custom_call_target="tpu_custom_call" | custom-call | tf_op jit(solution)/shard_map/pallas_call | solution.py:419
  31.5 0.9 %copy.8 = bf16[3,64,16,128]{3,2,1,0:T(8,128)(2,1)} copy(bf16[3,64,16,128]{3,2,1,0:T(8,128)(2,1)S(1)} %bitcast.7) | data formatting | bytes 1572864
